TPU v7x, 256 devices: a whole 4x4x8 slice. The times are simulated.
256 devices in a mesh: dap: 16 (over x, z_lo), cplx: 16 (over y, z_hi, core).
Axes of the slice: x: 4, y: 4, z: 8 (z_hi: 2, z_lo: 4; z = z_hi * 4 + z_lo), core: 2. Of those that a mesh axis runs over, the one named last changes fastest.
Arguments:
- pair: bfloat16 [192, 3072, 128], P('dap', 'cplx'), parts along dimension 1, may hold values from -6 to 6
- cotangent: bfloat16 [192, 3072, 128], P('dap', 'cplx'), parts along dimension 1, may hold values from -6 to 6
- residue_mask: int32 [3072], P('cplx'), parts along dimension 0, may hold values 0 or 1
- chain_ids: int32 [3072], P('cplx'), parts along dimension 0, may hold values from 0 to 2, never falling along the last dimension, each value on 1 to 96 neighbouring positions
- chain_embed: float32 [2, 128], replicated, may hold values from -4 to 4
- out_norm_gain: float32 [128], replicated, may hold values from 0.25 to 1.75
- out_proj: bfloat16 [128, 512], replicated, may hold values from -0.5 to 0.5
- out_gate: bfloat16 [128, 128], replicated, may hold values from -0.5 to 0.5
- out_mid_gain: float32 [128], replicated, may hold values from 0.25 to 1.75
- out_final: bfloat16 [128, 128], replicated, may hold values from -0.5 to 0.5
- in_norm_gain: float32 [128], replicated, may hold values from 0.25 to 1.75
- in_proj: bfloat16 [128, 512], replicated, may hold values from -0.5 to 0.5
- in_gate: bfloat16 [128, 128], replicated, may hold values from -0.5 to 0.5
- in_mid_gain: float32 [128], replicated, may hold values from 0.25 to 1.75
- in_final: bfloat16 [128, 128], replicated, may hold values from -0.5 to 0.5
Outputs:
- pair_grad: bfloat16 [192, 3072, 128], P('dap', 'cplx'), parts along dimension 1
- grad_proj: float32 [2048, 512], P('cplx'), parts along dimension 0
- grad_gate: float32 [2048, 128], P('cplx'), parts along dimension 0
- grad_final: float32 [2048, 128], P('cplx'), parts along dimension 0
- grad_norm_gain: float32 [2048], P('cplx'), parts along dimension 0
- grad_mid_gain: float32 [2048], P('cplx'), parts along dimension 0
There are 16 independent parts, one for each index of `cplx`. A program takes and returns all parts, laid end to end along the dimension named above; an argument that names none is the same for every part. Nothing has to cross between parts.
Inputs may be any that keep to these rules, and one draw needn't show every extreme that they name: `chain_ids`: chain numbers never fall along the residues; each chain has at most 96 residues.
All inputs are finite; a program needn't handle non-finite values.
Results may differ from a plain program's by a relative error of at most 0.019.
Values may be sent and summed in bfloat16 or wider, within the bound.
No kernel may reach another device: no remote copies, remote signals or barrier semaphores. Data moves between devices by JAX's collectives and lax.ppermute only.
A program may use at most 128 MiB of HBM per device.

v0:
```python
import jax
import jax.numpy as jnp
from jax import lax
from jax.sharding import PartitionSpec as P


def together(arrays, axis):
    ends = [0]
    for a in arrays:
        ends.append(ends[-1] + a.size)
    subtotal = lax.psum(jnp.concatenate([a.ravel() for a in arrays]), axis)
    return tuple((subtotal[b:e].reshape(a.shape) for a, b, e in zip(arrays, ends, ends[1:])))


def layer_norm(values_in, gain):
    average = jnp.mean(values_in, axis=-1, keepdims=True)
    centred = values_in - average
    variance = jnp.mean(centred * centred, axis=-1, keepdims=True)
    return centred * lax.rsqrt(variance + 1e-05) * gain


def gated_pair(projected, pair_mask, hidden_width):
    masked = pair_mask[..., None]
    left_act = (
        masked
        * jax.nn.sigmoid(projected[..., :hidden_width])
        * projected[..., hidden_width : 2 * hidden_width]
    )
    right_act = (
        masked
        * jax.nn.sigmoid(projected[..., 2 * hidden_width : 3 * hidden_width])
        * projected[..., 3 * hidden_width :]
    )
    return (left_act, right_act)


def shards(
    pair,
    cotangent,
    residue_mask,
    chain_ids,
    chain_embed,
    out_norm_gain,
    out_proj,
    out_gate,
    out_mid_gain,
    out_final,
    in_norm_gain,
    in_proj,
    in_gate,
    in_mid_gain,
    in_final,
):
    f32 = jnp.float32
    bf16 = jnp.bfloat16
    row_count = pair.shape[0]
    res_count = pair.shape[1]
    hidden_width = out_final.shape[0]
    inv_count = 1.0 / res_count
    row_start = lax.axis_index("dap") * row_count
    row_mask = lax.dynamic_slice_in_dim(residue_mask, row_start, row_count, 0)
    row_chain = lax.dynamic_slice_in_dim(chain_ids, row_start, row_count, 0)
    pair_mask = (row_mask[:, None] * residue_mask[None, :]).astype(f32)
    same_chain = row_chain[:, None] == chain_ids[None, :]
    start = pair.astype(f32) + jnp.where(same_chain[..., None], chain_embed[1], chain_embed[0])
    out_normed = layer_norm(start, out_norm_gain).astype(bf16)
    projected = jnp.dot(out_normed, out_proj, preferred_element_type=f32)
    left_act, right_act = gated_pair(projected, pair_mask, hidden_width)
    left_b = left_act.astype(bf16)
    right_b = right_act.astype(bf16)
    x_out = jnp.einsum(
        "ikc,jkc->ijc",
        left_b,
        lax.all_gather(right_b, "dap", axis=0, tiled=True),
        preferred_element_type=f32,
    )
    y_out = layer_norm(x_out, out_mid_gain).astype(bf16)
    update = jax.nn.sigmoid(jnp.dot(out_normed, out_gate, preferred_element_type=f32)) * jnp.dot(
        y_out, out_final, preferred_element_type=f32
    )
    pair_mid = (start + update).astype(bf16)
    mid_f32 = pair_mid.astype(f32)
    normed_f32, norm_back = jax.vjp(layer_norm, mid_f32, in_norm_gain)
    in_normed = normed_f32.astype(bf16)
    proj_in = jnp.dot(in_normed, in_proj, preferred_element_type=f32)
    (left_in, right_in), glu_back = jax.vjp(
        lambda proj_val: gated_pair(proj_val, pair_mask, hidden_width), proj_in
    )
    left_ib = left_in.astype(bf16)
    right_ib = right_in.astype(bf16)
    columns = lax.all_to_all(left_ib, "dap", split_axis=1, concat_axis=0, tiled=True)
    left_block = columns
    x_in = jnp.einsum(
        "kic,kjc->ijc",
        left_block,
        lax.all_gather(right_ib, "dap", axis=0, tiled=True),
        preferred_element_type=f32,
    )
    y_f32, mid_back = jax.vjp(layer_norm, x_in, in_mid_gain)
    y_in = y_f32.astype(bf16)
    logit = jnp.dot(in_normed, in_gate, preferred_element_type=f32)
    value = jnp.dot(y_in, in_final, preferred_element_type=f32)
    sigma = jax.nn.sigmoid(logit)
    upstream = cotangent.astype(f32)
    grad_value = (upstream * sigma).astype(bf16)
    grad_logit = (upstream * value * sigma * (1.0 - sigma)).astype(bf16)
    grad_final = jnp.einsum("ijc,ijd->cd", y_in, grad_value, preferred_element_type=f32) * inv_count
    grad_gate = (
        jnp.einsum("ijc,ijd->cd", in_normed, grad_logit, preferred_element_type=f32) * inv_count
    )
    grad_y = jnp.dot(grad_value, in_final.T, preferred_element_type=f32)
    grad_x, grad_mid = mid_back(grad_y)
    grad_x_b = grad_x.astype(bf16)
    shard_rows = lax.all_gather(grad_x_b, "dap", axis=0, tiled=True)
    left_block = left_ib
    grad_right = jnp.einsum("kic,ijc->kjc", left_block, shard_rows, preferred_element_type=f32)
    new_block = jnp.einsum("kjc,ijc->kic", right_ib, shard_rows, preferred_element_type=f32)
    grad_p = glu_back((new_block, grad_right))[0].astype(bf16)
    grad_proj = jnp.einsum("ijc,ijd->cd", in_normed, grad_p, preferred_element_type=f32) * inv_count
    grad_normed = jnp.dot(grad_p, in_proj.T, preferred_element_type=f32) + jnp.dot(
        grad_logit, in_gate.T, preferred_element_type=f32
    )
    grad_z, grad_norm = norm_back(grad_normed)
    pair_grad = (upstream + grad_z).astype(bf16)
    reduced = tuple(
        (
            part.astype(jnp.float32)
            for part in together(
                (
                    grad_proj.astype(jnp.bfloat16),
                    grad_gate.astype(jnp.bfloat16),
                    grad_final.astype(jnp.bfloat16),
                    (grad_norm * inv_count).astype(jnp.bfloat16),
                    (grad_mid * inv_count).astype(jnp.bfloat16),
                ),
                "dap",
            )
        )
    )
    return (pair_grad, reduced[0], reduced[1], reduced[2], reduced[3], reduced[4])


def solution(mesh):
    placed = (
        P("dap", "cplx", None),
        P("dap", "cplx", None),
        P("cplx"),
        P("cplx"),
        P(),
        P(),
        P(),
        P(),
        P(),
        P(),
        P(),
        P(),
        P(),
        P(),
        P(),
    )
    return jax.shard_map(
        shards,
        mesh=mesh,
        in_specs=placed,
        out_specs=(
            P("dap", "cplx", None),
            P("cplx", None),
            P("cplx", None),
            P("cplx", None),
            P("cplx"),
            P("cplx"),
        ),
        check_vma=False,
    )
```

profile of v0, /device:TPU:1, one launch (start us, length us, event | category | flops | bytes accessed | tf_op | source)
XLA Modules:
  0.0 922.6 jit_solution(3358620269729586650)
XLA Ops:
  11.6 2.3 multiply_reduce_fusion.4
  18.7 2.8 fusion.12
  21.5 205.2 %all-gather.4.cloned.1.call-done = bf16[192,192,128]{2,1,0:T(8,128)(2,1)} async-done(((bf16[12,192,128]{2,1,0:T(8,128)(2,1)}), bf16[192,192,128]{2,1,0:T(8,128)(2,1)}) %all-gather.4.cloned.1.call-update) | async-done | bytes 9437200 | tf_op jit(solution)/shard_map/all_gather | solution.py:74
  226.7 17.4 %copy.46 = bf16[192,192,128]{1,0,2:T(8,128)(2,1)} copy(bf16[192,192,128]{2,1,0:T(8,128)(2,1)} %all-gather.4.cloned.1.call-done) | data formatting | bytes 18874368 | tf_op jit(solution)/shard_map/all_gather | solution.py:74
  244.1 8.2 bitcast_reduce_fusion
  261.1 4.3 all-to-all-start
  266.5 36.2 %all-to-all-done = bf16[12,192,128]{2,0,1:T(8,128)(2,1)} async-done(((bf16[12,192,128]{2,0,1:T(8,128)(2,1)}), bf16[12,192,128]{2,0,1:T(8,128)(2,1)}, u32[]{:S(2)}, u32[]{:S(2)}) %all-to-all-start) | async-done | bytes 589856 | tf_op jit(solution)/shard_map/all_to_all | solution.py:91
  306.8 169.2 %all-gather.6.cloned.1.call-done = bf16[192,192,128]{2,1,0:T(8,128)(2,1)} async-done(((bf16[12,192,128]{2,1,0:T(8,128)(2,1)}), bf16[192,192,128]{2,1,0:T(8,128)(2,1)}) %all-gather.6.cloned.1.call-update) | async-done | bytes 9437200 | tf_op jit(solution)/shard_map/all_gather | solution.py:96
  476.0 17.4 %copy.52 = bf16[192,192,128]{1,0,2:T(8,128)(2,1)} copy(bf16[192,192,128]{2,1,0:T(8,128)(2,1)} %all-gather.6.cloned.1.call-done) | data formatting | bytes 18874368 | tf_op jit(solution)/shard_map/all_gather | solution.py:96
  493.4 7.6 fusion.82
  501.1 2.2 copy.54
  507.4 2.3 add_convert_fusion.1
  510.0 2.6 copy.59
  512.6 2.6 copy.56
  515.3 2.7 fusion.15
  518.0 198.0 %all-gather.8.cloned.1.call-done = bf16[192,192,128]{2,1,0:T(8,128)(2,1)} async-done(((bf16[12,192,128]{2,1,0:T(8,128)(2,1)}), bf16[192,192,128]{2,1,0:T(8,128)(2,1)}) %all-gather.8.cloned.1.call-update) | async-done | bytes 9437200 | tf_op jit(solution)/shard_map/all_gather | solution.py:114
  716.0 17.4 %copy.55 = bf16[192,192,128]{1,0,2:T(8,128)(2,1)} copy(bf16[192,192,128]{2,1,0:T(8,128)(2,1)} %all-gather.8.cloned.1.call-done) | data formatting | bytes 18874368 | tf_op jit(solution)/shard_map/all_gather | solution.py:114
  733.4 9.5 %fusion.84 = f32[128,192,12]{1,2,0:T(8,128)} fusion(bf16[192,192,128]{1,0,2:T(8,128)(2,1)} %copy.55, bf16[12,192,128]{1,0,2:T(8,128)(2,1)} %copy.59), kind=kOutput, calls=%fused_computation.145 | convolution fusion | flops 113246208 | bytes 11206656 | tf_op jit(solution)/shard_map/kjc,ijc->kic/dot_general | solution.py:117
  742.9 2.7 copy.60
  745.6 7.9 fusion.83
  753.5 2.7 copy.57
  756.2 3.7 bitcast_multiply_fusion.3
  768.1 2.5 fusion.22
  770.6 141.1 %all-reduce.6.cloned.1.call-done = bf16[98560]{0:T(1024)(128)(2,1)} async-done(((bf16[98560]{0:T(1024)(128)(2,1)}), bf16[98560]{0:T(1024)(128)(2,1)}) %all-reduce.6.cloned.1.call-update) | async-done | bytes 197136 | tf_op jit(solution)/shard_map/psum | solution.py:11
  (98 shorter events, 39.8 us)
Async XLA Ops:
  7.2 249.5 %copy-start = (bf16[128,512]{1,0:T(8,128)(2,1)S(1)}, bf16[128,512]{1,0:T(8,128)(2,1)}, u32[]{:S(2)}) copy-start(bf16[128,512]{1,0:T(8,128)(2,1)} %param.26) | copy-start | bytes 393220
  7.2 6.9 copy-start.5
  7.2 6.7 copy-start.16
  7.2 6.8 copy-start.18
  7.2 6.8 copy-start.11
  7.2 219.4 %all-gather.4.cloned.1.call-start = ((), (), s32[]{:S(2)}) async-start(), calls=%async_computation.1 | async-start | bytes 10027008 | tf_op jit(solution)/shard_map/all_gather | solution.py:74
  16.7 2.0 copy-start.19
  16.7 459.3 %all-gather.6.cloned.1.call-start = ((), (), s32[]{:S(2)}) async-start(), calls=%async_computation.2 | async-start | bytes 10027008 | tf_op jit(solution)/shard_map/all_gather | solution.py:96
  252.2 0.7 copy-start.17
  252.9 1.3 copy-start.8
  252.9 1.3 copy-start.12
  254.2 2.5 copy-start.15
  257.5 2.3 copy-start.1
  259.8 1.3 copy-start.6
  259.8 5.8 copy-start.13
  261.1 41.5 %all-to-all-start = ((bf16[12,192,128]{2,0,1:T(8,128)(2,1)}), bf16[12,192,128]{2,0,1:T(8,128)(2,1)}, u32[]{:S(2)}, u32[]{:S(2)}) async-start(bf16[12,192,128]{2,0,1:T(8,128)(2,1)} %copy.49), calls=%async_computation | async-start | bytes 1572864 | tf_op jit(solution)/shard_map/all_to_all | solution.py:91
  265.4 450.6 %all-gather.8.cloned.1.call-start = ((), (), s32[]{:S(2)}) async-start(), calls=%async_computation.3 | async-start | bytes 10027008 | tf_op jit(solution)/shard_map/all_gather | solution.py:114
  503.3 1.1 copy-start.2
  503.3 1.1 copy-start.10
  503.3 1.0 copy-start.14
  509.8 401.9 %all-reduce.6.cloned.1.call-start = ((), (), s32[]{:S(2)}) async-start(), calls=%async_computation.4 | async-start | bytes 397312 | tf_op jit(solution)/shard_map/psum | solution.py:11
  761.2 1.1 copy-start.7
  762.0 1.3 copy-start.3
  765.2 2.9 copy-start.4
  (1 other events, 0.7 us)
Sparse Core Ops, SparseCore 0:
  16.8 209.7 all-gather.3
  259.9 216.0 all-gather.5
  509.9 206.0 all-gather.7
  768.2 143.3 all-reduce.5
where the time goes:
time: 933 us; the launch traced here: 923 us
  waiting for transfers between devices  750 us (80%)
  local copies, waits for them, and re-layouts  78.5 us (8%)
  matrix products  49.2 us (5%)
  other arithmetic  26.1 us (3%)
  between operations  14.2 us (2%)
    all_gather x1, waiting for transfers between devices, shards(): lax.all_gather(right_b, 'dap', axis=0, tiled=True)  205 us
    all_gather x1, waiting for transfers between devices, shards(): shard_rows = lax.all_gather(grad_x_b, 'dap', axis=0, tiled=True)  198 us
    all_gather x1, waiting for transfers between devices, shards(): lax.all_gather(right_ib, 'dap', axis=0, tiled=True)  169 us
    psum x1, waiting for transfers between devices, together(): subtotal = lax.psum(jnp.concatenate([a.ravel() for a in arrays]), axis)  141 us
    all_to_all x1, waiting for transfers between devices, shards(): lax.all_to_all(left_ib, 'dap', split_axis=1, concat_axis=0, tiled=True)  36.2 us
  transfers between devices with their start and end apart: 5, of which 5 were waited for; matrix products, arithmetic and copies ran while one was open for 2% of the time, Pallas kernels for 0%

commit v1 on v0

v1 whole, which is shorter than its diff:
```python
import jax
import jax.numpy as jnp
from jax import lax
from jax.experimental import pallas as pl
from jax.experimental.pallas import tpu as pltpu
from jax.sharding import PartitionSpec as P

F32 = jnp.float32
BF16 = jnp.bfloat16
AXIS = "dap"
DEVS = 16
ROWS = 12
RES = 192
CH = 128
CPD = CH // DEVS
POS = ROWS * RES
TILE = 2 * RES
STEPS = POS // TILE
LANES = 128
LTILES = POS // LANES
GCOLS = 7 * CH
EPS = 1e-05


def dot_nn(a, b):
    return lax.dot_general(a, b, (((1,), (0,)), ((), ())), preferred_element_type=F32)


def dot_nt(a, b):
    return lax.dot_general(a, b, (((1,), (1,)), ((), ())), preferred_element_type=F32)


def dot_tn(a, b):
    return lax.dot_general(a, b, (((0,), (0,)), ((), ())), preferred_element_type=F32)


def column(row):
    block = jnp.transpose(jnp.broadcast_to(row, (CH, LANES)))
    return jnp.concatenate([block] * (TILE // LANES), axis=1)


def sigmoid(v):
    return 1.0 / (1.0 + jnp.exp(-v))


def stats(v):
    centred = v - jnp.mean(v, axis=0, keepdims=True)
    variance = jnp.mean(centred * centred, axis=0, keepdims=True)
    return centred, lax.rsqrt(variance + EPS)


def norm_grad(hat, rstd, gain, grad):
    h = grad * gain
    return rstd * (
        h - jnp.mean(h, axis=0, keepdims=True) - hat * jnp.mean(h * hat, axis=0, keepdims=True)
    )


def tile_rows(first_ref, table_ref, step):
    base = first_ref[0] + 2 * step
    lane = lax.broadcasted_iota(jnp.int32, (1, TILE), 1)
    return jnp.where(lane < RES, table_ref[base], table_ref[base + 1])


def tile_mask(first_ref, mask_ref, lanes_ref, step):
    return (tile_rows(first_ref, mask_ref, step) * lanes_ref[0:1, :]).astype(F32)


def interleave(left, right):
    n = left.shape[1]
    both = jnp.stack([left.reshape(DEVS, CPD, n), right.reshape(DEVS, CPD, n)], axis=1)
    return both.reshape(DEVS, 2 * CPD, n)


def lane_sums(v):
    return sum(v[:, i * LANES : (i + 1) * LANES] for i in range(v.shape[1] // LANES))


def first_kernel(first, mask, chain, lanes, pair, embed, gain, proj, gate, send, start, gated):
    step = pl.program_id(0)
    pm = tile_mask(first, mask, lanes, step)
    same = tile_rows(first, chain, step) == lanes[1:2, :]
    values = jnp.transpose(pair[...].astype(F32).reshape(TILE, CH))
    values = values + jnp.where(same, column(embed[1:2, :]), column(embed[0:1, :]))
    start[...] = values
    centred, rstd = stats(values)
    normed = (centred * rstd * column(gain[...])).astype(BF16)
    p = dot_tn(proj[...], normed)
    left = pm * sigmoid(p[:CH]) * p[CH : 2 * CH]
    right = pm * sigmoid(p[2 * CH : 3 * CH]) * p[3 * CH :]
    send[...] = interleave(left, right).astype(BF16)
    gated[...] = sigmoid(dot_tn(gate[...], normed))


def middle_kernel(
    first, mask, lanes, xs, start, gated, mid_gain, final, gain, proj, send, pair_mid, in_normed
):
    step = pl.program_id(0)
    pm = tile_mask(first, mask, lanes, step)
    centred, rstd = stats(xs[...].astype(F32).reshape(CH, TILE))
    y = (centred * rstd * column(mid_gain[...])).astype(BF16)
    mid = (start[...] + gated[...] * dot_tn(final[...], y)).astype(BF16)
    pair_mid[...] = mid
    centred, rstd = stats(mid.astype(F32))
    normed = (centred * rstd * column(gain[...])).astype(BF16)
    in_normed[...] = normed
    p = dot_tn(proj[...], normed)
    left = pm * sigmoid(p[:CH]) * p[CH : 2 * CH]
    right = pm * sigmoid(p[2 * CH : 3 * CH]) * p[3 * CH :]
    send[...] = interleave(left, right).astype(BF16)


def turn_kernel(xs, cot, in_normed, mid_gain, gate, final, send, grad_logit, sums):
    step = pl.program_id(0)
    gain = column(mid_gain[...])
    centred, rstd = stats(xs[...].astype(F32).reshape(CH, TILE))
    hat = centred * rstd
    y = (hat * gain).astype(BF16)
    normed = in_normed[...]
    sigma = sigmoid(dot_tn(gate[...], normed))
    value = dot_tn(final[...], y)
    upstream = jnp.transpose(cot[...].astype(F32).reshape(TILE, CH))
    grad_value = (upstream * sigma).astype(BF16)
    grad_lg = (upstream * value * sigma * (1.0 - sigma)).astype(BF16)
    grad_logit[...] = grad_lg
    grad_y = dot_nn(final[...], grad_value)
    send[...] = norm_grad(hat, rstd, gain, grad_y).astype(BF16).reshape(DEVS, CPD, TILE)

    @pl.when(step == 0)
    def _():
        sums[...] = jnp.zeros_like(sums)

    sums[:, :CH] += dot_nt(normed, grad_lg)
    sums[:, CH : 2 * CH] += dot_nt(y, grad_value)
    sums[:, 2 * CH :] += lane_sums(grad_y * hat)


def last_kernel(
    first, mask, lanes, gs, cot, in_normed, pair_mid, grad_logit, gain_row, proj, gate, sums,
    pair_grad, packed, acc_proj, acc_gain,
):
    step = pl.program_id(0)
    pm = tile_mask(first, mask, lanes, step)
    normed = in_normed[...]
    p = dot_tn(proj[...], normed)
    grads = gs[...].astype(F32).reshape(DEVS, 2, CPD, TILE)
    parts = []
    for side in range(2):
        grad = pm * grads[:, side].reshape(CH, TILE)
        sig = sigmoid(p[2 * side * CH : (2 * side + 1) * CH])
        val = p[(2 * side + 1) * CH : (2 * side + 2) * CH]
        parts.append((grad * val * sig * (1.0 - sig)).astype(BF16))
        parts.append((grad * sig).astype(BF16))
    grad_p = jnp.concatenate(parts, axis=0)
    grad_normed = dot_nn(proj[...], grad_p) + dot_nn(gate[...], grad_logit[...])
    centred, rstd = stats(pair_mid[...].astype(F32))
    hat = centred * rstd
    grad_z = norm_grad(hat, rstd, column(gain_row[...]), grad_normed)
    out = cot[...].astype(F32).reshape(TILE, CH) + jnp.transpose(grad_z)
    pair_grad[...] = out.astype(BF16).reshape(2, RES, CH)

    @pl.when(step == 0)
    def _():
        acc_proj[...] = jnp.zeros_like(acc_proj)
        acc_gain[...] = jnp.zeros_like(acc_gain)

    acc_proj[...] += dot_nt(normed, grad_p)
    acc_gain[...] += lane_sums(grad_normed * hat)

    @pl.when(step == STEPS - 1)
    def _():
        lane = lax.broadcasted_iota(jnp.int32, (CH, LANES), 1)
        norm_sum = jnp.sum(acc_gain[...], axis=1, keepdims=True)
        mid_sum = jnp.sum(sums[:, 2 * CH :], axis=1, keepdims=True)
        gains = jnp.where(lane == 0, norm_sum, jnp.where(lane == 1, mid_sum, 0.0))
        full = jnp.concatenate([acc_proj[...], sums[:, : 2 * CH], gains], axis=1)
        packed[...] = (full * (1.0 / RES)).astype(BF16).reshape(DEVS, CPD, GCOLS)


def add_kernel(parts, out):
    total = jnp.sum(parts[...].astype(F32), axis=0).astype(BF16)
    out[...] = jnp.broadcast_to(total[None], out.shape)


def unpack_kernel(parts, proj, gate, final, gains):
    full = parts[...].astype(F32).reshape(CH, GCOLS)
    proj[...] = full[:, : 4 * CH]
    gate[...] = full[:, 4 * CH : 5 * CH]
    final[...] = full[:, 5 * CH : 6 * CH]
    gains[...] = jnp.transpose(full[:, 6 * CH :])[:8]


def unfold(recv, flat, width):
    rows = DEVS * width
    for t in range(LTILES):
        block = recv[:, :, t * LANES : (t + 1) * LANES].astype(F32)
        flat[t * rows : (t + 1) * rows, :] = block.reshape(rows, LANES)


def fold(flat, send, width):
    rows = DEVS * width
    for t in range(LTILES):
        block = flat[t * rows : (t + 1) * rows, :].reshape(DEVS, width, LANES)
        send[:, :, t * LANES : (t + 1) * LANES] = block.astype(BF16)


def low_half():
    return lax.broadcasted_iota(jnp.int32, (DEVS, LANES), 1) < LANES // 2


def gather_matrix(flat, width, c, mat):
    rows = DEVS * width
    low = low_half()
    for q in range(STEPS):
        t0, t1, t2 = (
            flat[pl.ds((3 * q + h) * rows + c, DEVS, stride=width), :] for h in range(3)
        )
        r1 = pltpu.roll(t1, LANES // 2, axis=1)
        r2 = pltpu.roll(t2, LANES // 2, axis=1)
        mat[pl.ds(2 * q, DEVS, stride=ROWS), :] = t0
        mat[pl.ds(RES + 2 * q, DEVS, stride=ROWS), :] = t1
        mat[pl.ds(2 * q + 1, DEVS, stride=ROWS), :] = jnp.where(low, r1, r2)
        mat[pl.ds(RES + 2 * q + 1, DEVS, stride=ROWS), :] = r2
    full = jnp.concatenate([mat[:RES, :], mat[RES:, :]], axis=1)
    return full[:, :RES].astype(BF16)


def scatter_matrix(value, mat, flat, width, c):
    rows = DEVS * width
    low = low_half()
    mat[:RES, :] = value[:, :LANES]
    mat[RES:, : RES - LANES] = value[:, LANES:]
    for q in range(STEPS):
        e0 = mat[pl.ds(2 * q, DEVS, stride=ROWS), :]
        e1 = mat[pl.ds(RES + 2 * q, DEVS, stride=ROWS), :]
        o0 = pltpu.roll(mat[pl.ds(2 * q + 1, DEVS, stride=ROWS), :], LANES // 2, axis=1)
        o1 = pltpu.roll(mat[pl.ds(RES + 2 * q + 1, DEVS, stride=ROWS), :], LANES // 2, axis=1)
        tiles = (e0, jnp.where(low, e1, o0), jnp.where(low, o0, o1))
        for h in range(3):
            flat[pl.ds((3 * q + h) * rows + c, DEVS, stride=width), :] = tiles[h]


def outgoing_kernel(recv, send, flat, mat_a, mat_b, out):
    unfold(recv, flat, 2 * CPD)
    for c in range(CPD):
        a = gather_matrix(flat, 2 * CPD, c, mat_a)
        b = gather_matrix(flat, 2 * CPD, CPD + c, mat_b)
        scatter_matrix(dot_nt(a, b), mat_a, out, CPD, c)
    fold(out, send, CPD)


def incoming_kernel(recv, send, sides, flat, mat_a, mat_b, out):
    unfold(recv, flat, 2 * CPD)
    for c in range(CPD):
        a = gather_matrix(flat, 2 * CPD, c, mat_a)
        b = gather_matrix(flat, 2 * CPD, CPD + c, mat_b)
        sides[c] = a
        sides[CPD + c] = b
        scatter_matrix(dot_tn(a, b), mat_a, out, CPD, c)
    fold(out, send, CPD)


def backward_kernel(recv, sides, send, flat, mat_a, mat_b, out):
    unfold(recv, flat, CPD)
    for c in range(CPD):
        g = gather_matrix(flat, CPD, c, mat_a)
        scatter_matrix(dot_nt(sides[CPD + c], g), mat_a, out, 2 * CPD, c)
        scatter_matrix(dot_nn(sides[c], g), mat_b, out, 2 * CPD, CPD + c)
    fold(out, send, 2 * CPD)


def product(kernel, args, out_shape, width_in, width_out, name):
    return pl.pallas_call(
        kernel,
        out_shape=out_shape,
        scratch_shapes=[
            pltpu.VMEM((LTILES * DEVS * width_in, LANES), F32),
            pltpu.VMEM((2 * RES, LANES), F32),
            pltpu.VMEM((2 * RES, LANES), F32),
            pltpu.VMEM((LTILES * DEVS * width_out, LANES), F32),
        ],
        name=name,
    )(*args)


SMEM = pl.BlockSpec(memory_space=pltpu.SMEM)


def whole(shape):
    return pl.BlockSpec(shape, lambda i: (0,) * len(shape))


def tiled(*lead):
    return pl.BlockSpec((*lead, TILE), lambda i: (0,) * len(lead) + (i,))


ROW_BLOCK = pl.BlockSpec((2, RES, CH), lambda i: (i, 0, 0))
GAIN = whole((1, CH))
LANE_INFO = whole((2, TILE))


def over_tiles(kernel, args, in_specs, out_specs, out_shape, name, scratch=()):
    return pl.pallas_call(
        kernel,
        grid=(STEPS,),
        in_specs=in_specs,
        out_specs=out_specs,
        out_shape=out_shape,
        scratch_shapes=scratch,
        name=name,
    )(*args)


def shaped(shape, dtype=BF16):
    return jax.ShapeDtypeStruct(shape, dtype)


def exchange(v):
    return lax.all_to_all(v, AXIS, 0, 0)


def shards(
    pair,
    cotangent,
    residue_mask,
    chain_ids,
    chain_embed,
    out_norm_gain,
    out_proj,
    out_gate,
    out_mid_gain,
    out_final,
    in_norm_gain,
    in_proj,
    in_gate,
    in_mid_gain,
    in_final,
):
    first = (lax.axis_index(AXIS) * ROWS).astype(jnp.int32).reshape(1)
    info = jnp.stack([residue_mask, chain_ids])
    info = jnp.concatenate([info, info], axis=1)
    gains = [g.reshape(1, CH) for g in (out_norm_gain, out_mid_gain, in_norm_gain, in_mid_gain)]
    square = whole((CH, CH))
    wide = whole((CH, 4 * CH))
    pair_send = shaped((DEVS, 2 * CPD, POS))
    one_send = shaped((DEVS, CPD, POS))

    send, start, gated = over_tiles(
        first_kernel,
        (first, residue_mask, chain_ids, info, pair, chain_embed, gains[0], out_proj, out_gate),
        [SMEM, SMEM, SMEM, LANE_INFO, ROW_BLOCK, whole((2, CH)), GAIN, wide, square],
        [tiled(DEVS, 2 * CPD), tiled(CH), tiled(CH)],
        [pair_send, shaped((CH, POS), F32), shaped((CH, POS), F32)],
        "first",
    )
    x_out = product(outgoing_kernel, (exchange(send),), one_send, 2 * CPD, CPD, "outgoing")
    send, pair_mid, in_normed = over_tiles(
        middle_kernel,
        (first, residue_mask, info, exchange(x_out), start, gated, gains[1], out_final, gains[2], in_proj),
        [SMEM, SMEM, LANE_INFO, tiled(DEVS, CPD), tiled(CH), tiled(CH), GAIN, square, GAIN, wide],
        [tiled(DEVS, 2 * CPD), tiled(CH), tiled(CH)],
        [pair_send, shaped((CH, POS)), shaped((CH, POS))],
        "middle",
    )
    x_in, sides = product(
        incoming_kernel,
        (exchange(send),),
        [one_send, shaped((2 * CPD, RES, RES))],
        2 * CPD,
        CPD,
        "incoming",
    )
    send, grad_logit, sums = over_tiles(
        turn_kernel,
        (exchange(x_in), cotangent, in_normed, gains[3], in_gate, in_final),
        [tiled(DEVS, CPD), ROW_BLOCK, tiled(CH), GAIN, square, square],
        [tiled(DEVS, CPD), tiled(CH), whole((CH, 3 * CH))],
        [one_send, shaped((CH, POS)), shaped((CH, 3 * CH), F32)],
        "turn",
    )
    grads = product(backward_kernel, (exchange(send), sides), pair_send, CPD, 2 * CPD, "backward")
    pair_grad, packed = over_tiles(
        last_kernel,
        (first, residue_mask, info, exchange(grads), cotangent, in_normed, pair_mid, grad_logit,
         gains[2], in_proj, in_gate, sums),
        [SMEM, SMEM, LANE_INFO, tiled(DEVS, 2 * CPD), ROW_BLOCK, tiled(CH), tiled(CH), tiled(CH),
         GAIN, wide, square, whole((CH, 3 * CH))],
        [ROW_BLOCK, whole((DEVS, CPD, GCOLS))],
        [shaped((ROWS, RES, CH)), shaped((DEVS, CPD, GCOLS))],
        "last",
        [pltpu.VMEM((CH, 4 * CH), F32), pltpu.VMEM((CH, LANES), F32)],
    )
    total = pl.pallas_call(add_kernel, out_shape=shaped((DEVS, CPD, GCOLS)), name="add")(
        exchange(packed)
    )
    grad_proj, grad_gate, grad_final, grad_gains = pl.pallas_call(
        unpack_kernel,
        out_shape=[shaped((CH, 4 * CH), F32), shaped((CH, CH), F32), shaped((CH, CH), F32), shaped((8, CH), F32)],
        name="unpack",
    )(exchange(total))
    return pair_grad, grad_proj, grad_gate, grad_final, grad_gains[0], grad_gains[1]


def solution(mesh):
    rows = P("dap", "cplx", None)
    return jax.shard_map(
        shards,
        mesh=mesh,
        in_specs=(rows, rows, P("cplx"), P("cplx")) + (P(),) * 11,
        out_specs=(
            rows,
            P("cplx", None),
            P("cplx", None),
            P("cplx", None),
            P("cplx"),
            P("cplx"),
        ),
        check_vma=False,
    )
```

time: 933 us -> 249 us (0.27)
  waiting for transfers between devices: 750 us -> 0 us
  blocking collectives: 0 us -> 197 us
  local copies, waits for them, and re-layouts: 78.5 us -> 1.27 us
  matrix products: 49.2 us -> 0 us
  Pallas kernels: 0 us -> 45.2 us
  other arithmetic: 26.1 us -> 1.41 us
  between operations: 14.2 us -> 0.65 us
    all_gather x3 -> x0, waiting for transfers between devices: 572 us -> none  [the longest x1 205 us: shards(): lax.all_gather(right_b, 'dap', axis=0, tiled=True)]
    all_to_all x0 -> x8, blocking collectives: none -> 197 us  [exchange(): return lax.all_to_all(v, AXIS, 0, 0)]
    psum x1 -> x0, waiting for transfers between devices: 141 us -> none  [together(): subtotal = lax.psum(jnp.concatenate([a.ravel() for a in arrays]), axis)]
    all_gather x3 -> x0, local copies, waits for them, and re-layouts: 52.2 us -> none  [the longest x1 17.4 us: shards(): lax.all_gather(right_b, 'dap', axis=0, tiled=True)]
    dot_general x16 -> x0, matrix products: 49.2 us -> none  [the longest x1 9.51 us: shards(): jnp.einsum('kjc,ijc->kic', right_ib, shard_rows, preferred_element_type=f32)]
    pallas_call x0 -> x9, Pallas kernels: none -> 45.2 us  [the longest x4 27.8 us: over_tiles(): pl.pallas_call(kernel, grid=(STEPS,), in_specs=in_specs, out_specs=out_sp...]
    all_to_all x1 -> x0, waiting for transfers between devices: 36.2 us -> none  [shards(): lax.all_to_all(left_ib, 'dap', split_axis=1, concat_axis=0, tiled=True)]
    convert_element_type x11 -> x0, other arithmetic: 12.2 us -> none  [the longest x3 3.61 us: shards(): part.astype(jnp.float32)]
  transfers between devices with their start and end apart: 5 -> 0, of which waited for: 5 -> 0; matrix products, arithmetic and copies ran while one was open for 2% -> 0% of each run, Pallas kernels for 0% -> 0%
where the time goes in v1:
time: 249 us; the launch traced here: 246 us
  blocking collectives  197 us (79%)
  Pallas kernels  45.2 us (18%)
    all_to_all x8, blocking collectives, exchange(): return lax.all_to_all(v, AXIS, 0, 0)  197 us
    pallas_call x4, Pallas kernels, over_tiles(): pl.pallas_call(kernel, grid=(STEPS,), in_specs=in_specs, out_specs=out_sp...  27.8 us
    pallas_call x3, Pallas kernels, product(): pl.pallas_call(kernel, out_shape=out_shape, scratch_shapes=[pltpu.VMEM((L...  14.1 us

profile of v1, /device:TPU:1, one launch (start us, length us, event | category | flops | bytes accessed | tf_op | source)
XLA Modules:
  0.0 245.9 jit_solution(5314614711300274850)
XLA Ops:
  0.6 1.4 add_add_fusion.lanes
  2.0 6.0 %first.1 = (bf16[16,16,2304]{2,1,0:T(8,128)(2,1)}, f32[128,2304]{1,0:T(8,128)}, f32[128,2304]{1,0:T(8,128)}) custom-call(s32[1]{0:T(128)} %bitcast.first, s32[192]{0:T(256)} %mask.5, s32[192]{0:T(256)} %chain.1, s32[2,384]{1,0:T(2,128)} %add_add_fusion.lanes, bf16[12,192,128]{2,1,0:T(8,128)(2,1)} %pair.1, f32[2,128]{1,0:T(2,128)} %embed.1, ...), custom_call_target="tpu_custom_call" | custom-call | tf_op jit(solution)/shard_map/first/pallas_call | solution.py:303
  8.0 39.2 %all_to_all.40.recv = bf16[16,16,2304]{2,1,0:T(8,128)(2,1)} all-to-all(bf16[16,16,2304]{2,1,0:T(8,128)(2,1)} %get-tuple-element.23), channel_id=1, replica_groups=mesh['dap'=16,'cplx'=16] {'dap'}, dimensions={0} | all-to-all | bytes 2359296 | tf_op jit(solution)/shard_map/all_to_all | solution.py:319
  47.2 4.3 %outgoing.1 = bf16[16,8,2304]{2,1,0:T(8,128)(2,1)} custom-call(bf16[16,16,2304]{2,1,0:T(8,128)(2,1)} %all_to_all.40.recv), custom_call_target="tpu_custom_call" | custom-call | tf_op jit(solution)/shard_map/outgoing/pallas_call | solution.py:273
  51.5 21.4 %all_to_all.41.xs = bf16[16,8,2304]{2,1,0:T(8,128)(2,1)} all-to-all(bf16[16,8,2304]{2,1,0:T(8,128)(2,1)} %outgoing.1), channel_id=1, replica_groups=mesh['dap'=16,'cplx'=16] {'dap'}, dimensions={0} | all-to-all | bytes 1179648 | tf_op jit(solution)/shard_map/all_to_all | solution.py:319
  72.9 6.9 %middle.1 = (bf16[16,16,2304]{2,1,0:T(8,128)(2,1)}, bf16[128,2304]{1,0:T(8,128)(2,1)}, bf16[128,2304]{1,0:T(8,128)(2,1)}) custom-call(s32[1]{0:T(128)} %bitcast.first, s32[192]{0:T(256)} %mask.5, s32[2,384]{1,0:T(2,128)} %add_add_fusion.lanes, bf16[16,8,2304]{2,1,0:T(8,128)(2,1)} %all_to_all.41.xs, f32[128,2304]{1,0:T(8,128)} %get-tuple-element.24.start, ...), custom_call_target="tpu_custom_call" | custom-call | tf_op jit(solution)/shard_map/middle/pallas_call | solution.py:303
  79.8 34.5 %all_to_all.42.recv = bf16[16,16,2304]{2,1,0:T(8,128)(2,1)} all-to-all(bf16[16,16,2304]{2,1,0:T(8,128)(2,1)} %get-tuple-element.26), channel_id=1, replica_groups=mesh['dap'=16,'cplx'=16] {'dap'}, dimensions={0} | all-to-all | bytes 2359296 | tf_op jit(solution)/shard_map/all_to_all | solution.py:319
  114.3 4.7 %incoming.1 = (bf16[16,8,2304]{2,1,0:T(8,128)(2,1)}, bf16[16,192,192]{2,1,0:T(8,128)(2,1)}) custom-call(bf16[16,16,2304]{2,1,0:T(8,128)(2,1)} %all_to_all.42.recv), custom_call_target="tpu_custom_call" | custom-call | tf_op jit(solution)/shard_map/incoming/pallas_call | solution.py:273
  119.0 21.4 %all_to_all.43.xs = bf16[16,8,2304]{2,1,0:T(8,128)(2,1)} all-to-all(bf16[16,8,2304]{2,1,0:T(8,128)(2,1)} %get-tuple-element.27), channel_id=1, replica_groups=mesh['dap'=16,'cplx'=16] {'dap'}, dimensions={0} | all-to-all | bytes 1179648 | tf_op jit(solution)/shard_map/all_to_all | solution.py:319
  140.4 6.5 %turn.1 = (bf16[16,8,2304]{2,1,0:T(8,128)(2,1)}, bf16[128,2304]{1,0:T(8,128)(2,1)}, f32[128,384]{1,0:T(8,128)}) custom-call(bf16[16,8,2304]{2,1,0:T(8,128)(2,1)} %all_to_all.43.xs, bf16[12,192,128]{2,1,0:T(8,128)(2,1)} %cot.3, bf16[128,2304]{1,0:T(8,128)(2,1)} %get-tuple-element.28.in_normed, f32[1,128]{1,0:T(1,128)} %bitcast.17, bf16[128,128]{1,0:T(8,128)(2,1)} %gate.5, ...), custom_call_target="tpu_custom_call" | custom-call | tf_op jit(solution)/shard_map/turn/pallas_call | solution.py:303
  146.9 21.4 %all_to_all.44.recv = bf16[16,8,2304]{2,1,0:T(8,128)(2,1)} all-to-all(bf16[16,8,2304]{2,1,0:T(8,128)(2,1)} %get-tuple-element.29), channel_id=1, replica_groups=mesh['dap'=16,'cplx'=16] {'dap'}, dimensions={0} | all-to-all | bytes 1179648 | tf_op jit(solution)/shard_map/all_to_all | solution.py:319
  168.3 5.1 %backward.1 = bf16[16,16,2304]{2,1,0:T(8,128)(2,1)} custom-call(bf16[16,8,2304]{2,1,0:T(8,128)(2,1)} %all_to_all.44.recv, bf16[16,192,192]{2,1,0:T(8,128)(2,1)} %get-tuple-element.30.sides), custom_call_target="tpu_custom_call" | custom-call | tf_op jit(solution)/shard_map/backward/pallas_call | solution.py:273
  173.4 34.5 %all_to_all.45.gs = bf16[16,16,2304]{2,1,0:T(8,128)(2,1)} all-to-all(bf16[16,16,2304]{2,1,0:T(8,128)(2,1)} %backward.1), channel_id=1, replica_groups=mesh['dap'=16,'cplx'=16] {'dap'}, dimensions={0} | all-to-all | bytes 2359296 | tf_op jit(solution)/shard_map/all_to_all | solution.py:319
  207.9 8.4 %last.1 = (bf16[12,192,128]{2,1,0:T(8,128)(2,1)}, bf16[16,8,896]{2,1,0:T(8,128)(2,1)}) custom-call(s32[1]{0:T(128)} %bitcast.first, s32[192]{0:T(256)} %mask.5, s32[2,384]{1,0:T(2,128)} %add_add_fusion.lanes, bf16[16,16,2304]{2,1,0:T(8,128)(2,1)} %all_to_all.45.gs, bf16[12,192,128]{2,1,0:T(8,128)(2,1)} %cot.3, ...), custom_call_target="tpu_custom_call" | custom-call | tf_op jit(solution)/shard_map/last/pallas_call | solution.py:303
  216.3 12.3 %all_to_all.46.parts = bf16[16,8,896]{2,1,0:T(8,128)(2,1)} all-to-all(bf16[16,8,896]{2,1,0:T(8,128)(2,1)} %get-tuple-element.35), channel_id=1, replica_groups=mesh['dap'=16,'cplx'=16] {'dap'}, dimensions={0} | all-to-all | bytes 458752 | tf_op jit(solution)/shard_map/all_to_all | solution.py:319
  228.7 1.7 add.7
  230.3 12.6 %all_to_all.47.parts = bf16[16,8,896]{2,1,0:T(8,128)(2,1)} all-to-all(bf16[16,8,896]{2,1,0:T(8,128)(2,1)} %add.7), channel_id=1, replica_groups=mesh['dap'=16,'cplx'=16] {'dap'}, dimensions={0} | all-to-all | bytes 458752 | tf_op jit(solution)/shard_map/all_to_all | solution.py:319
  242.9 1.7 unpack.1
  244.6 1.3 slice_bitcast_fusion

commit v2 on v1

v2 whole, which is shorter than its diff:
```python
import jax
import jax.numpy as jnp
from jax import lax
from jax.experimental import pallas as pl
from jax.experimental.pallas import tpu as pltpu
from jax.sharding import PartitionSpec as P

F32 = jnp.float32
BF16 = jnp.bfloat16
AXIS = "dap"
DEVS = 16
ROWS = 12
RES = 192
CH = 128
CPD = CH // DEVS
POS = ROWS * RES
TROWS = 6
TILE = TROWS * RES
STEPS = POS // TILE
LANES = 128
LTILES = POS // LANES
GCOLS = 6 * CH
EPS = 1e-05


def dot_nn(a, b):
    return lax.dot_general(a, b, (((1,), (0,)), ((), ())), preferred_element_type=F32)


def dot_nt(a, b):
    return lax.dot_general(a, b, (((1,), (1,)), ((), ())), preferred_element_type=F32)


def dot_tn(a, b):
    return lax.dot_general(a, b, (((0,), (0,)), ((), ())), preferred_element_type=F32)


def column(row):
    block = jnp.transpose(jnp.broadcast_to(row, (CH, LANES)))
    return jnp.concatenate([block] * (TILE // LANES), axis=1)


def sigmoid(v):
    return 0.5 + 0.5 * jnp.tanh(0.5 * v)


def stats(v):
    centred = v - jnp.mean(v, axis=0, keepdims=True)
    variance = jnp.mean(centred * centred, axis=0, keepdims=True)
    return centred, lax.rsqrt(variance + EPS)


def norm_grad(hat, rstd, h):
    return rstd * (
        h - jnp.mean(h, axis=0, keepdims=True) - hat * jnp.mean(h * hat, axis=0, keepdims=True)
    )


def window(step):
    return pl.ds(pl.multiple_of(step * TILE, TILE), TILE)


def tile_rows(first_ref, table_ref, step):
    base = first_ref[0] + TROWS * step
    lane = lax.broadcasted_iota(jnp.int32, (1, TILE), 1)
    out = jnp.full((1, TILE), table_ref[base], jnp.int32)
    for r in range(1, TROWS):
        out = jnp.where(lane < r * RES, out, table_ref[base + r])
    return out


def along_lanes(row_ref, wide_ref):
    wide_ref[...] = jnp.zeros_like(wide_ref)
    wide_ref[:1, :RES] = row_ref[...]
    row = wide_ref[...]
    lane = lax.broadcasted_iota(jnp.int32, row.shape, 1)
    double = jnp.where(lane < RES, row, pltpu.roll(row, RES, axis=1))[0:1]
    return jnp.concatenate([double] * (TROWS // 2), axis=1)


def tile_mask(first_ref, mask_ref, row_ref, wide_ref, step):
    return (tile_rows(first_ref, mask_ref, step) * along_lanes(row_ref, wide_ref)).astype(F32)


def interleave(left, right):
    n = left.shape[1]
    both = jnp.stack([left.reshape(DEVS, CPD, n), right.reshape(DEVS, CPD, n)], axis=1)
    return both.reshape(DEVS, 2 * CPD, n)


def lane_sums(v):
    return sum(v[:, i * LANES : (i + 1) * LANES] for i in range(v.shape[1] // LANES))


def turned(block):
    return jnp.transpose(block.astype(F32).reshape(TILE, CH))


def gated_pair(pm, p):
    left = pm * sigmoid(p[:CH]) * p[CH : 2 * CH]
    right = pm * sigmoid(p[2 * CH : 3 * CH]) * p[3 * CH :]
    return interleave(left, right).astype(BF16)


def first_kernel(
    first, mask, chain, mask_row, chain_row, pair, embed, gain, proj, send, start, normed_out, wide
):
    step = pl.program_id(0)
    pm = tile_mask(first, mask, mask_row, wide, step)
    same = tile_rows(first, chain, step) == along_lanes(chain_row, wide)
    values = turned(pair[...])
    values = values + jnp.where(same, column(embed[1:2, :]), column(embed[0:1, :]))
    start[...] = values
    centred, rstd = stats(values)
    normed = (centred * rstd * column(gain[...])).astype(BF16)
    normed_out[...] = normed
    send[:, :, window(step)] = gated_pair(pm, dot_tn(proj[...], normed))


def gate_kernel(normed, gate, gated):
    gated[...] = sigmoid(dot_tn(gate[...], normed[...]))


def middle_kernel(
    first, mask, mask_row, xs, start, gated, mid_gain, final, gain, proj, send, pair_mid, in_normed,
    wide,
):
    step = pl.program_id(0)
    pm = tile_mask(first, mask, mask_row, wide, step)
    centred, rstd = stats(xs[:, :, window(step)].astype(F32).reshape(CH, TILE))
    y = (centred * rstd * column(mid_gain[...])).astype(BF16)
    mid = (start[...] + gated[...] * dot_tn(final[...], y)).astype(BF16)
    pair_mid[...] = mid
    centred, rstd = stats(mid.astype(F32))
    normed = (centred * rstd * column(gain[...])).astype(BF16)
    in_normed[...] = normed
    send[:, :, window(step)] = gated_pair(pm, dot_tn(proj[...], normed))


def ahead_kernel(first, mask, mask_row, cot, in_normed, gain, gate, final, proj,
                 grad_value, grad_h, factor, factors, wide):
    step = pl.program_id(0)
    pm = tile_mask(first, mask, mask_row, wide, step)
    normed = in_normed[...]
    sigma = sigmoid(dot_tn(gate[...], normed))
    upstream = turned(cot[...])
    scaled = upstream * sigma
    rounded = scaled.astype(BF16)
    grad_value[...] = rounded
    factor[...] = scaled * (1.0 - sigma)
    grad_h[...] = dot_nn(final[...], rounded) * column(gain[...])
    p = dot_tn(proj[...], normed)
    for side in range(2):
        low = 2 * side * CH
        raw = sigmoid(p[low : low + CH])
        sig = pm * raw
        factors[low : low + CH, :] = (sig * p[low + CH : low + 2 * CH] * (1.0 - raw)).astype(BF16)
        factors[low + CH : low + 2 * CH, :] = sig.astype(BF16)


def turn_kernel(xs, grad_h, send):
    step = pl.program_id(0)
    centred, rstd = stats(xs[:, :, window(step)].astype(F32).reshape(CH, TILE))
    grad_x = norm_grad(centred * rstd, rstd, grad_h[...])
    send[:, :, window(step)] = grad_x.astype(BF16).reshape(DEVS, CPD, TILE)


def after_kernel(xs, in_normed, grad_value, factor, gain, final, gate, sums, from_gate):
    step = pl.program_id(0)
    centred, rstd = stats(xs[:, :, window(step)].astype(F32).reshape(CH, TILE))
    hat = centred * rstd
    y = (hat * column(gain[...])).astype(BF16)
    normed = in_normed[...]
    rounded = grad_value[...]
    grad_logit = (factor[...] * dot_tn(final[...], y)).astype(BF16)
    grad_y = dot_nn(final[...], rounded)
    from_gate[...] = dot_nn(gate[...], grad_logit)

    @pl.when(step == 0)
    def _():
        sums[...] = jnp.zeros_like(sums)

    sums[:, :CH] += dot_nt(normed, grad_logit)
    sums[:, CH : 2 * CH] += dot_nt(y, rounded)
    sums[:, 2 * CH :] += lane_sums(grad_y * hat)


def last_kernel(gs, in_normed, factors, sums, grad_p, packed, acc_proj):
    step = pl.program_id(0)
    grads = gs[:, :, window(step)].astype(F32).reshape(DEVS, 2, CPD, TILE)
    for side in range(2):
        grad = grads[:, side].reshape(CH, TILE)
        for part in range(2):
            low = (2 * side + part) * CH
            grad_p[low : low + CH, :] = (grad * factors[low : low + CH, :].astype(F32)).astype(BF16)

    @pl.when(step == 0)
    def _():
        acc_proj[...] = jnp.zeros_like(acc_proj)

    acc_proj[...] += dot_nt(in_normed[...], grad_p[...])

    @pl.when(step == STEPS - 1)
    def _():
        full = jnp.concatenate([acc_proj[...], sums[:, : 2 * CH]], axis=1)
        packed[...] = (full * (1.0 / RES)).astype(BF16).reshape(DEVS, CPD, GCOLS)


def norm_kernel(cot, pair_mid, grad_p, from_gate, gain, proj, sums, pair_grad, gains, acc):
    step = pl.program_id(0)
    grad_normed = dot_nn(proj[...], grad_p[...]) + from_gate[...]
    centred, rstd = stats(pair_mid[...].astype(F32))
    hat = centred * rstd
    grad_z = norm_grad(hat, rstd, grad_normed * column(gain[...]))
    out = cot[...].astype(F32).reshape(TILE, CH) + jnp.transpose(grad_z)
    pair_grad[...] = out.astype(BF16).reshape(TROWS, RES, CH)

    @pl.when(step == 0)
    def _():
        acc[...] = jnp.zeros_like(acc)

    acc[...] += lane_sums(grad_normed * hat)

    @pl.when(step == STEPS - 1)
    def _():
        norm_row = jnp.sum(jnp.transpose(acc[...]), axis=0, keepdims=True)
        mid_row = jnp.sum(jnp.transpose(sums[:, 2 * CH :]), axis=0, keepdims=True)
        index = lax.broadcasted_iota(jnp.int32, (CPD, CH), 0)
        rows = jnp.where(index == 0, norm_row, jnp.where(index == 1, mid_row, 0.0))
        gains[...] = rows * (1.0 / RES)


def add_kernel(parts, gains, out):
    total = jnp.sum(parts[...].astype(F32), axis=0)
    total = jnp.concatenate([total, gains[...]], axis=1).astype(BF16)
    out[...] = jnp.broadcast_to(total[None], out.shape)


def unpack_kernel(parts, proj, gate, final, norm_gain, mid_gain):
    full = parts[:, :, :GCOLS].astype(F32).reshape(CH, GCOLS)
    proj[...] = full[:, : 4 * CH]
    gate[...] = full[:, 4 * CH : 5 * CH]
    final[...] = full[:, 5 * CH :]
    gains = jnp.sum(parts[:, :, GCOLS:].astype(F32), axis=0)
    norm_gain[...] = gains[0:1]
    mid_gain[...] = gains[1:2]


def unfold(recv, flat, width):
    rows = DEVS * width
    for t in range(LTILES):
        block = recv[:, :, t * LANES : (t + 1) * LANES].astype(F32)
        flat[t * rows : (t + 1) * rows, :] = block.reshape(rows, LANES)


def fold(flat, send, width):
    rows = DEVS * width
    for t in range(LTILES):
        block = flat[t * rows : (t + 1) * rows, :].reshape(DEVS, width, LANES)
        send[:, :, t * LANES : (t + 1) * LANES] = block.astype(BF16)


def low_half():
    return lax.broadcasted_iota(jnp.int32, (DEVS, LANES), 1) < LANES // 2


def gather_matrix(flat, width, c, mat):
    rows = DEVS * width
    low = low_half()
    for q in range(ROWS // 2):
        t0, t1, t2 = (
            flat[pl.ds((3 * q + h) * rows + c, DEVS, stride=width), :] for h in range(3)
        )
        r1 = pltpu.roll(t1, LANES // 2, axis=1)
        r2 = pltpu.roll(t2, LANES // 2, axis=1)
        mat[pl.ds(2 * q, DEVS, stride=ROWS), :] = t0
        mat[pl.ds(RES + 2 * q, DEVS, stride=ROWS), :] = t1
        mat[pl.ds(2 * q + 1, DEVS, stride=ROWS), :] = jnp.where(low, r1, r2)
        mat[pl.ds(RES + 2 * q + 1, DEVS, stride=ROWS), :] = r2
    full = jnp.concatenate([mat[:RES, :], mat[RES:, :]], axis=1)
    return full[:, :RES].astype(BF16)


def scatter_matrix(value, mat, flat, width, c):
    rows = DEVS * width
    low = low_half()
    mat[:RES, :] = value[:, :LANES]
    mat[RES:, : RES - LANES] = value[:, LANES:]
    for q in range(ROWS // 2):
        e0 = mat[pl.ds(2 * q, DEVS, stride=ROWS), :]
        e1 = mat[pl.ds(RES + 2 * q, DEVS, stride=ROWS), :]
        o0 = pltpu.roll(mat[pl.ds(2 * q + 1, DEVS, stride=ROWS), :], LANES // 2, axis=1)
        o1 = pltpu.roll(mat[pl.ds(RES + 2 * q + 1, DEVS, stride=ROWS), :], LANES // 2, axis=1)
        tiles = (e0, jnp.where(low, e1, o0), jnp.where(low, o0, o1))
        for h in range(3):
            flat[pl.ds((3 * q + h) * rows + c, DEVS, stride=width), :] = tiles[h]


def outgoing_kernel(recv, send, flat, mats_a, mats_b, out):
    unfold(recv, flat, 2 * CPD)
    for c in range(CPD):
        a = gather_matrix(flat, 2 * CPD, c, mats_a.at[c])
        b = gather_matrix(flat, 2 * CPD, CPD + c, mats_b.at[c])
        scatter_matrix(dot_nt(a, b), mats_a.at[c], out, CPD, c)
    fold(out, send, CPD)


def incoming_kernel(recv, send, sides, flat, mats_a, mats_b, out):
    unfold(recv, flat, 2 * CPD)
    for c in range(CPD):
        a = gather_matrix(flat, 2 * CPD, c, mats_a.at[c])
        b = gather_matrix(flat, 2 * CPD, CPD + c, mats_b.at[c])
        sides[c] = a
        sides[CPD + c] = b
        scatter_matrix(dot_tn(a, b), mats_a.at[c], out, CPD, c)
    fold(out, send, CPD)


def backward_kernel(recv, sides, send, flat, mats_a, mats_b, out):
    unfold(recv, flat, CPD)
    for c in range(CPD):
        g = gather_matrix(flat, CPD, c, mats_a.at[c])
        scatter_matrix(dot_nt(sides[CPD + c], g), mats_a.at[c], out, 2 * CPD, c)
        scatter_matrix(dot_nn(sides[c], g), mats_b.at[c], out, 2 * CPD, CPD + c)
    fold(out, send, 2 * CPD)


def product(kernel, args, out_shape, width_in, width_out, name):
    return pl.pallas_call(
        kernel,
        out_shape=out_shape,
        scratch_shapes=[
            pltpu.VMEM((LTILES * DEVS * width_in, LANES), F32),
            pltpu.VMEM((CPD, 2 * RES, LANES), F32),
            pltpu.VMEM((CPD, 2 * RES, LANES), F32),
            pltpu.VMEM((LTILES * DEVS * width_out, LANES), F32),
        ],
        name=name,
    )(*args)


SMEM = pl.BlockSpec(memory_space=pltpu.SMEM)
HERE = pl.BlockSpec(memory_space=pltpu.VMEM)


def whole(shape):
    return pl.BlockSpec(shape, lambda i: (0,) * len(shape))


def tiled(*lead):
    return pl.BlockSpec((*lead, TILE), lambda i: (0,) * len(lead) + (i,))


ROW_BLOCK = pl.BlockSpec((TROWS, RES, CH), lambda i: (i, 0, 0))
GAIN = whole((1, CH))
LANE_INFO = whole((1, RES))
WIDE_ROW = [pltpu.VMEM((8, 2 * RES), jnp.int32)]
SQUARE = whole((CH, CH))
WIDE = whole((CH, 4 * CH))
COLS = tiled(CH)


def over_tiles(kernel, args, in_specs, out_specs, out_shape, name, scratch=()):
    return pl.pallas_call(
        kernel,
        grid=(STEPS,),
        in_specs=in_specs,
        out_specs=out_specs,
        out_shape=out_shape,
        scratch_shapes=scratch,
        cost_estimate=pl.CostEstimate(flops=1 << 30, bytes_accessed=1 << 22, transcendentals=0),
        name=name,
    )(*args)


def shaped(shape, dtype=BF16):
    return jax.ShapeDtypeStruct(shape, dtype)


def near(shape, dtype=BF16):
    return pltpu.VMEM(shape, dtype)


def exchange(v):
    return pltpu.with_memory_space_constraint(lax.all_to_all(v, AXIS, 0, 0), pltpu.VMEM)


def shards(
    pair,
    cotangent,
    residue_mask,
    chain_ids,
    chain_embed,
    out_norm_gain,
    out_proj,
    out_gate,
    out_mid_gain,
    out_final,
    in_norm_gain,
    in_proj,
    in_gate,
    in_mid_gain,
    in_final,
):
    first = (lax.axis_index(AXIS) * ROWS).astype(jnp.int32).reshape(1)
    mask_row, chain_row = residue_mask.reshape(1, RES), chain_ids.reshape(1, RES)
    gains = [g.reshape(1, CH) for g in (out_norm_gain, out_mid_gain, in_norm_gain, in_mid_gain)]
    pair_send = near((DEVS, 2 * CPD, POS))
    one_send = near((DEVS, CPD, POS))
    cols = shaped((CH, POS))
    cols_f32 = shaped((CH, POS), F32)

    send, start, out_normed = over_tiles(
        first_kernel,
        (first, residue_mask, chain_ids, mask_row, chain_row, pair, chain_embed, gains[0], out_proj),
        [SMEM, SMEM, SMEM, LANE_INFO, LANE_INFO, ROW_BLOCK, whole((2, CH)), GAIN, WIDE],
        [HERE, COLS, COLS],
        [pair_send, cols_f32, cols],
        "first",
        WIDE_ROW,
    )
    recv = exchange(send)
    gated = over_tiles(
        gate_kernel, (out_normed, out_gate), [COLS, SQUARE], COLS, cols_f32, "gate"
    )
    x_out = product(outgoing_kernel, (recv,), one_send, 2 * CPD, CPD, "outgoing")
    send, pair_mid, in_normed = over_tiles(
        middle_kernel,
        (first, residue_mask, mask_row, exchange(x_out), start, gated, gains[1], out_final, gains[2], in_proj),
        [SMEM, SMEM, LANE_INFO, HERE, COLS, COLS, GAIN, SQUARE, GAIN, WIDE],
        [HERE, COLS, COLS],
        [pair_send, cols, cols],
        "middle",
        WIDE_ROW,
    )
    recv = exchange(send)
    grad_value, grad_h, factor, factors = over_tiles(
        ahead_kernel,
        (first, residue_mask, mask_row, cotangent, in_normed, gains[3], in_gate, in_final, in_proj),
        [SMEM, SMEM, LANE_INFO, ROW_BLOCK, COLS, GAIN, SQUARE, SQUARE, WIDE],
        [COLS, COLS, COLS, tiled(4 * CH)],
        [cols, cols_f32, cols_f32, shaped((4 * CH, POS))],
        "ahead",
        WIDE_ROW,
    )
    x_in, sides = product(
        incoming_kernel,
        (recv,),
        [one_send, near((2 * CPD, RES, RES))],
        2 * CPD,
        CPD,
        "incoming",
    )
    recv = exchange(x_in)
    send = over_tiles(turn_kernel, (recv, grad_h), [HERE, COLS], HERE, one_send, "turn")
    recv_x = exchange(send)
    sums, from_gate = over_tiles(
        after_kernel,
        (recv, in_normed, grad_value, factor, gains[3], in_final, in_gate),
        [HERE, COLS, COLS, COLS, GAIN, SQUARE, SQUARE],
        [whole((CH, 3 * CH)), COLS],
        [shaped((CH, 3 * CH), F32), cols_f32],
        "after",
    )
    grads = product(backward_kernel, (recv_x, sides), pair_send, CPD, 2 * CPD, "backward")
    grad_p, packed = over_tiles(
        last_kernel,
        (exchange(grads), in_normed, factors, sums),
        [HERE, COLS, tiled(4 * CH), whole((CH, 3 * CH))],
        [tiled(4 * CH), HERE],
        [shaped((4 * CH, POS)), near((DEVS, CPD, GCOLS))],
        "last",
        [pltpu.VMEM((CH, 4 * CH), F32)],
    )
    parts = exchange(packed)
    pair_grad, gain_rows = over_tiles(
        norm_kernel,
        (cotangent, pair_mid, grad_p, from_gate, gains[2], in_proj, sums),
        [ROW_BLOCK, COLS, tiled(4 * CH), COLS, GAIN, WIDE, whole((CH, 3 * CH))],
        [ROW_BLOCK, whole((CPD, CH))],
        [shaped((ROWS, RES, CH)), shaped((CPD, CH), F32)],
        "norm",
        [pltpu.VMEM((CH, LANES), F32)],
    )
    total = pl.pallas_call(
        add_kernel, out_shape=near((DEVS, CPD, GCOLS + CH)), name="add"
    )(parts, gain_rows)
    row = shaped((1, CH), F32)
    grad_proj, grad_gate, grad_final, grad_norm, grad_mid = pl.pallas_call(
        unpack_kernel,
        out_shape=[shaped((CH, 4 * CH), F32), shaped((CH, CH), F32), shaped((CH, CH), F32), row, row],
        name="unpack",
    )(exchange(total))
    return pair_grad, grad_proj, grad_gate, grad_final, grad_norm.reshape(CH), grad_mid.reshape(CH)


def solution(mesh):
    rows = P("dap", "cplx", None)
    return jax.shard_map(
        shards,
        mesh=mesh,
        in_specs=(rows, rows, P("cplx"), P("cplx")) + (P(),) * 11,
        out_specs=(
            rows,
            P("cplx", None),
            P("cplx", None),
            P("cplx", None),
            P("cplx"),
            P("cplx"),
        ),
        check_vma=False,
    )
```

time: 249 us -> 221 us (0.89)
  blocking collectives: 197 us -> 106 us
  waiting for transfers between devices: 0 us -> 56.8 us
  starting transfers between devices: 0 us -> 15.6 us
  Pallas kernels: 45.2 us -> 39.5 us
    all_to_all x8 -> x4, blocking collectives: 197 us -> 106 us  [exchange(): lax.all_to_all(v, AXIS, 0, 0)]
    all_to_all x0 -> x4, waiting for transfers between devices: none -> 56.8 us  [exchange(): lax.all_to_all(v, AXIS, 0, 0)]
    all_to_all x0 -> x4, starting transfers between devices: none -> 15.6 us  [exchange(): lax.all_to_all(v, AXIS, 0, 0)]
    pallas_call x3, Pallas kernels: 14.1 us -> 10.2 us  [product(): pl.pallas_call(kernel, out_shape=out_shape, scratch_shapes=[pltpu.VMEM((L...]
    pallas_call x4 -> x8, Pallas kernels: 27.8 us -> 27.9 us  [over_tiles(): pl.pallas_call(kernel, grid=(STEPS,), in_specs=in_specs, out_specs=out_sp...]
  transfers between devices with their start and end apart: 0 -> 4, of which waited for: 0 -> 4; matrix products, arithmetic and copies ran while one was open for 0% -> 0% of each run, Pallas kernels for 0% -> 7%
where the time goes in v2:
time: 221 us; the launch traced here: 218 us
  blocking collectives  106 us (48%)
  waiting for transfers between devices  56.8 us (26%)
  Pallas kernels  39.5 us (18%)
  starting transfers between devices  15.6 us (7%)
    all_to_all x4, blocking collectives, exchange(): lax.all_to_all(v, AXIS, 0, 0)  106 us
    all_to_all x4, waiting for transfers between devices, exchange(): lax.all_to_all(v, AXIS, 0, 0)  56.8 us
    pallas_call x8, Pallas kernels, over_tiles(): pl.pallas_call(kernel, grid=(STEPS,), in_specs=in_specs, out_specs=out_sp...  27.9 us
    all_to_all x4, starting transfers between devices, exchange(): lax.all_to_all(v, AXIS, 0, 0)  15.6 us
    pallas_call x3, Pallas kernels, product(): pl.pallas_call(kernel, out_shape=out_shape, scratch_shapes=[pltpu.VMEM((L...  10.2 us
  transfers between devices with their start and end apart: 4, of which 4 were waited for; matrix products, arithmetic and copies ran while one was open for 0% of the time, Pallas kernels for 7%

profile of v2, /device:TPU:1, one launch (start us, length us, event | category | flops | bytes accessed | tf_op | source)
XLA Modules:
  0.0 218.4 jit_solution(11375166075212293287)
XLA Ops:
  0.6 3.1 %first.1 = (bf16[16,16,2304]{2,1,0:T(8,128)(2,1)S(1)}, f32[128,2304]{1,0:T(8,128)}, bf16[128,2304]{1,0:T(8,128)(2,1)}) custom-call(s32[1]{0:T(128)} %bitcast.first, s32[192]{0:T(256)} %mask.5, s32[192]{0:T(256)} %chain.1, s32[1,192]{1,0:T(1,128)} %bitcast.12, s32[1,192]{1,0:T(1,128)} %bitcast.11, bf16[12,192,128]{2,1,0:T(8,128)(2,1)} %pair.1, ...), custom_call_target="tpu_custom_call" | custom-call | flops 1073741824 | bytes 4194304 | tf_op jit(solution)/shard_map/first/pallas_call | solution.py:364
  3.7 38.9 %all_to_all.40.recv = bf16[16,16,2304]{2,1,0:T(8,128)(2,1)S(1)} all-to-all(bf16[16,16,2304]{2,1,0:T(8,128)(2,1)S(1)} %get-tuple-element.29), channel_id=1, replica_groups=mesh['dap'=16,'cplx'=16] {'dap'}, dimensions={0} | all-to-all | bytes 2359296 | tf_op jit(solution)/shard_map/all_to_all | solution.py:385
  42.6 2.4 %outgoing.1 = bf16[16,8,2304]{2,1,0:T(8,128)(2,1)} custom-call(bf16[16,16,2304]{2,1,0:T(8,128)(2,1)S(1)} %all_to_all.40.recv), custom_call_target="tpu_custom_call" | custom-call | tf_op jit(solution)/shard_map/outgoing/pallas_call | solution.py:329
  45.0 3.6 %all-to-all-start.1 = ((bf16[16,8,2304]{2,1,0:T(8,128)(2,1)}), bf16[16,8,2304]{2,1,0:T(8,128)(2,1)S(1)}, u32[]{:S(2)}, u32[]{:S(2)}) async-start(bf16[16,8,2304]{2,1,0:T(8,128)(2,1)} %outgoing.1), calls=%async_computation.1 | async-start | bytes 1179648 | tf_op jit(solution)/shard_map/all_to_all | solution.py:385
  48.6 2.4 %gate.4.gated = f32[128,2304]{1,0:T(8,128)} custom-call(bf16[128,2304]{1,0:T(8,128)(2,1)} %get-tuple-element.31.normed, bf16[128,128]{1,0:T(8,128)(2,1)} %gate.5), custom_call_target="tpu_custom_call" | custom-call | flops 1073741824 | bytes 4194304 | tf_op jit(solution)/shard_map/gate/pallas_call | solution.py:364
  51.1 14.7 %all-to-all-done.1.xs = bf16[16,8,2304]{2,1,0:T(8,128)(2,1)S(1)} async-done(((bf16[16,8,2304]{2,1,0:T(8,128)(2,1)}), bf16[16,8,2304]{2,1,0:T(8,128)(2,1)S(1)}, u32[]{:S(2)}, u32[]{:S(2)}) %all-to-all-start.1) | async-done | bytes 589856 | tf_op jit(solution)/shard_map/all_to_all | solution.py:385
  65.8 3.8 %middle.1 = (bf16[16,16,2304]{2,1,0:T(8,128)(2,1)S(1)}, bf16[128,2304]{1,0:T(8,128)(2,1)}, bf16[128,2304]{1,0:T(8,128)(2,1)}) custom-call(s32[1]{0:T(128)} %bitcast.first, s32[192]{0:T(256)} %mask.5, s32[1,192]{1,0:T(1,128)} %bitcast.13, bf16[16,8,2304]{2,1,0:T(8,128)(2,1)S(1)} %all-to-all-done.1.xs, f32[128,2304]{1,0:T(8,128)} %get-tuple-element.30.start, ...), custom_call_target="tpu_custom_call" | custom-call | flops 1073741824 | bytes 4194304 | tf_op jit(solution)/shard_map/middle/pallas_call | solution.py:364
  69.5 33.3 %all_to_all.41.recv = bf16[16,16,2304]{2,1,0:T(8,128)(2,1)S(1)} all-to-all(bf16[16,16,2304]{2,1,0:T(8,128)(2,1)S(1)} %get-tuple-element.33), channel_id=1, replica_groups=mesh['dap'=16,'cplx'=16] {'dap'}, dimensions={0} | all-to-all | bytes 2359296 | tf_op jit(solution)/shard_map/all_to_all | solution.py:385
  102.8 3.6 %incoming.1 = (bf16[16,8,2304]{2,1,0:T(8,128)(2,1)}, bf16[16,192,192]{2,1,0:T(8,128)(2,1)S(1)}) custom-call(bf16[16,16,2304]{2,1,0:T(8,128)(2,1)S(1)} %all_to_all.41.recv), custom_call_target="tpu_custom_call" | custom-call | tf_op jit(solution)/shard_map/incoming/pallas_call | solution.py:329
  106.5 3.6 %all-to-all-start.3 = ((bf16[16,8,2304]{2,1,0:T(8,128)(2,1)}), bf16[16,8,2304]{2,1,0:T(8,128)(2,1)S(1)}, u32[]{:S(2)}, u32[]{:S(2)}) async-start(bf16[16,8,2304]{2,1,0:T(8,128)(2,1)} %get-tuple-element.34), calls=%async_computation.3 | async-start | bytes 1179648 | tf_op jit(solution)/shard_map/all_to_all | solution.py:385
  110.1 4.3 %ahead.1 = (bf16[128,2304]{1,0:T(8,128)(2,1)}, f32[128,2304]{1,0:T(8,128)}, f32[128,2304]{1,0:T(8,128)}, bf16[512,2304]{1,0:T(8,128)(2,1)}) custom-call(s32[1]{0:T(128)} %bitcast.first, s32[192]{0:T(256)} %mask.5, s32[1,192]{1,0:T(1,128)} %bitcast.14, bf16[12,192,128]{2,1,0:T(8,128)(2,1)} %cot.3, bf16[128,2304]{1,0:T(8,128)(2,1)} %get-tuple-element.35.in_normed, ...), custom_call_target="tpu_custom_call" | custom-call | flops 1073741824 | bytes 4194304 | tf_op jit(solution)/shard_map/ahead/pallas_call | solution.py:364
  114.3 12.9 %all-to-all-done.3.xs = bf16[16,8,2304]{2,1,0:T(8,128)(2,1)S(1)} async-done(((bf16[16,8,2304]{2,1,0:T(8,128)(2,1)}), bf16[16,8,2304]{2,1,0:T(8,128)(2,1)S(1)}, u32[]{:S(2)}, u32[]{:S(2)}) %all-to-all-start.3) | async-done | bytes 589856 | tf_op jit(solution)/shard_map/all_to_all | solution.py:385
  127.2 2.1 turn.1
  129.3 20.4 %all_to_all.42.recv = bf16[16,8,2304]{2,1,0:T(8,128)(2,1)S(1)} all-to-all(bf16[16,8,2304]{2,1,0:T(8,128)(2,1)S(1)} %turn.1), channel_id=1, replica_groups=mesh['dap'=16,'cplx'=16] {'dap'}, dimensions={0} | all-to-all | bytes 1179648 | tf_op jit(solution)/shard_map/all_to_all | solution.py:385
  149.7 4.1 %backward.1 = bf16[16,16,2304]{2,1,0:T(8,128)(2,1)} custom-call(bf16[16,8,2304]{2,1,0:T(8,128)(2,1)S(1)} %all_to_all.42.recv, bf16[16,192,192]{2,1,0:T(8,128)(2,1)} %copy-done), custom_call_target="tpu_custom_call" | custom-call | tf_op jit(solution)/shard_map/backward/pallas_call | solution.py:329
  153.8 4.0 %all-to-all-start.5 = ((bf16[16,16,2304]{2,1,0:T(8,128)(2,1)}), bf16[16,16,2304]{2,1,0:T(8,128)(2,1)S(1)}, u32[]{:S(2)}, u32[]{:S(2)}) async-start(bf16[16,16,2304]{2,1,0:T(8,128)(2,1)} %backward.1), calls=%async_computation.5 | async-start | bytes 2359296 | tf_op jit(solution)/shard_map/all_to_all | solution.py:385
  157.8 4.0 %after.1 = (f32[128,384]{1,0:T(8,128)}, f32[128,2304]{1,0:T(8,128)}) custom-call(bf16[16,8,2304]{2,1,0:T(8,128)(2,1)S(1)} %copy-done.2, bf16[128,2304]{1,0:T(8,128)(2,1)} %get-tuple-element.35.in_normed, bf16[128,2304]{1,0:T(8,128)(2,1)} %get-tuple-element.39.grad_value, f32[128,2304]{1,0:T(8,128)} %get-tuple-element.40.factor, f32[1,128]{1,0:T(1,128)} %bitcast.18, ...), custom_call_target="tpu_custom_call" | custom-call | flops 1073741824 | bytes 4194304 | tf_op jit(solution)/shard_map/after/pallas_call | solution.py:364
  161.8 25.9 %all-to-all-done.5.gs = bf16[16,16,2304]{2,1,0:T(8,128)(2,1)S(1)} async-done(((bf16[16,16,2304]{2,1,0:T(8,128)(2,1)}), bf16[16,16,2304]{2,1,0:T(8,128)(2,1)S(1)}, u32[]{:S(2)}, u32[]{:S(2)}) %all-to-all-start.5) | async-done | bytes 1179680 | tf_op jit(solution)/shard_map/all_to_all | solution.py:385
  187.7 4.1 %last.1 = (bf16[512,2304]{1,0:T(8,128)(2,1)}, bf16[16,8,768]{2,1,0:T(8,128)(2,1)}) custom-call(bf16[16,16,2304]{2,1,0:T(8,128)(2,1)S(1)} %all-to-all-done.5.gs, bf16[128,2304]{1,0:T(8,128)(2,1)} %get-tuple-element.35.in_normed, bf16[512,2304]{1,0:T(8,128)(2,1)} %get-tuple-element.38.factors, f32[128,384]{1,0:T(8,128)} %get-tuple-element.41.sums), custom_call_target="tpu_custom_call" | custom-call | flops 1073741824 | bytes 4194304 | tf_op jit(solution)/shard_map/last/pallas_call | solution.py:364
  191.8 4.5 %all-to-all-start.6 = ((bf16[16,8,768]{2,1,0:T(8,128)(2,1)}), bf16[16,8,768]{2,1,0:T(8,128)(2,1)S(1)}, u32[]{:S(2)}, u32[]{:S(2)}) async-start(bf16[16,8,768]{2,1,0:T(8,128)(2,1)} %get-tuple-element.45), calls=%async_computation.6 | async-start | bytes 393216 | tf_op jit(solution)/shard_map/all_to_all | solution.py:385
  196.3 4.2 %norm.1 = (bf16[12,192,128]{2,1,0:T(8,128)(2,1)}, f32[8,128]{1,0:T(8,128)}) custom-call(bf16[12,192,128]{2,1,0:T(8,128)(2,1)} %cot.3, bf16[128,2304]{1,0:T(8,128)(2,1)} %get-tuple-element.32.pair_mid, bf16[512,2304]{1,0:T(8,128)(2,1)} %get-tuple-element.42.grad_p, f32[128,2304]{1,0:T(8,128)} %get-tuple-element.43.from_gate, f32[1,128]{1,0:T(1,128)} %bitcast.10, ...), custom_call_target="tpu_custom_call" | custom-call | flops 1073741824 | bytes 4194304 | tf_op jit(solution)/shard_map/norm/pallas_call | solution.py:364
  200.5 3.3 %all-to-all-done.6.parts = bf16[16,8,768]{2,1,0:T(8,128)(2,1)S(1)} async-done(((bf16[16,8,768]{2,1,0:T(8,128)(2,1)}), bf16[16,8,768]{2,1,0:T(8,128)(2,1)S(1)}, u32[]{:S(2)}, u32[]{:S(2)}) %all-to-all-start.6) | async-done | bytes 196640 | tf_op jit(solution)/shard_map/all_to_all | solution.py:385
  204.6 13.1 %all_to_all.43.parts = bf16[16,8,896]{2,1,0:T(8,128)(2,1)S(1)} all-to-all(bf16[16,8,896]{2,1,0:T(8,128)(2,1)S(1)} %add.1), channel_id=1, replica_groups=mesh['dap'=16,'cplx'=16] {'dap'}, dimensions={0} | all-to-all | bytes 458752 | tf_op jit(solution)/shard_map/all_to_all | solution.py:385
  217.6 0.8 unpack.1
  (7 shorter events, 0.7 us)
Async XLA Ops:
  45.0 20.7 %all-to-all-start.1 = ((bf16[16,8,2304]{2,1,0:T(8,128)(2,1)}), bf16[16,8,2304]{2,1,0:T(8,128)(2,1)S(1)}, u32[]{:S(2)}, u32[]{:S(2)}) async-start(bf16[16,8,2304]{2,1,0:T(8,128)(2,1)} %outgoing.1), calls=%async_computation.1 | async-start | bytes 1179648 | tf_op jit(solution)/shard_map/all_to_all | solution.py:385
  106.5 7.9 %copy-start = (bf16[16,192,192]{2,1,0:T(8,128)(2,1)}, bf16[16,192,192]{2,1,0:T(8,128)(2,1)S(1)}, u32[]{:S(2)}) copy-start(bf16[16,192,192]{2,1,0:T(8,128)(2,1)S(1)} %get-tuple-element.37.sides) | copy-start | bytes 3538948
  106.5 20.7 %all-to-all-start.3 = ((bf16[16,8,2304]{2,1,0:T(8,128)(2,1)}), bf16[16,8,2304]{2,1,0:T(8,128)(2,1)S(1)}, u32[]{:S(2)}, u32[]{:S(2)}) async-start(bf16[16,8,2304]{2,1,0:T(8,128)(2,1)} %get-tuple-element.34), calls=%async_computation.3 | async-start | bytes 1179648 | tf_op jit(solution)/shard_map/all_to_all | solution.py:385
  127.2 2.1 copy-start.1
  153.8 4.0 %copy-start.2 = (bf16[16,8,2304]{2,1,0:T(8,128)(2,1)S(1)}, bf16[16,8,2304]{2,1,0:T(8,128)(2,1)}, u32[]{:S(2)}) copy-start(bf16[16,8,2304]{2,1,0:T(8,128)(2,1)} %copy-done.1) | copy-start | bytes 1769476
  153.8 33.8 %all-to-all-start.5 = ((bf16[16,16,2304]{2,1,0:T(8,128)(2,1)}), bf16[16,16,2304]{2,1,0:T(8,128)(2,1)S(1)}, u32[]{:S(2)}, u32[]{:S(2)}) async-start(bf16[16,16,2304]{2,1,0:T(8,128)(2,1)} %backward.1), calls=%async_computation.5 | async-start | bytes 2359296 | tf_op jit(solution)/shard_map/all_to_all | solution.py:385
  191.8 12.0 %all-to-all-start.6 = ((bf16[16,8,768]{2,1,0:T(8,128)(2,1)}), bf16[16,8,768]{2,1,0:T(8,128)(2,1)S(1)}, u32[]{:S(2)}, u32[]{:S(2)}) async-start(bf16[16,8,768]{2,1,0:T(8,128)(2,1)} %get-tuple-element.45), calls=%async_computation.6 | async-start | bytes 393216 | tf_op jit(solution)/shard_map/all_to_all | solution.py:385

commit v3 on v2

--- a/solution.py
+++ b/solution.py
@@ -20,6 +20,7 @@
 LANES = 128
 LTILES = POS // LANES
 GCOLS = 6 * CH
+HOLD_NS = {"first": (0, 14700), "outgoing": (1000, 0), "middle": (0, 3600)}
 EPS = 1e-05
 
 
@@ -102,23 +103,41 @@
     return interleave(left, right).astype(BF16)
 
 
+def hold(first_ref, name, step=0):
+    for core, nanos in enumerate(HOLD_NS[name]):
+        if nanos:
+
+            @pl.when((step == 0) & (first_ref[1] == core))
+            def _():
+                pl.delay(nanos)
+
+
+def with_chains(first, chain, chain_row, pair, embed, wide, step):
+    same = tile_rows(first, chain, step) == along_lanes(chain_row, wide)
+    return turned(pair[...]) + jnp.where(same, column(embed[1:2, :]), column(embed[0:1, :]))
+
+
+def normed_by(values, gain):
+    centred, rstd = stats(values)
+    return (centred * rstd * column(gain[...])).astype(BF16)
+
+
 def first_kernel(
-    first, mask, chain, mask_row, chain_row, pair, embed, gain, proj, send, start, normed_out, wide
+    first, mask, chain, mask_row, chain_row, pair, embed, gain, proj, send, wide
 ):
     step = pl.program_id(0)
+    hold(first, "first", step)
     pm = tile_mask(first, mask, mask_row, wide, step)
-    same = tile_rows(first, chain, step) == along_lanes(chain_row, wide)
-    values = turned(pair[...])
-    values = values + jnp.where(same, column(embed[1:2, :]), column(embed[0:1, :]))
+    values = with_chains(first, chain, chain_row, pair, embed, wide, step)
+    normed = normed_by(values, gain)
+    send[:, :, window(step)] = gated_pair(pm, dot_tn(proj[...], normed))
+
+
+def gate_kernel(first, chain, chain_row, pair, embed, gain, gate, start, gated, wide):
+    step = pl.program_id(0)
+    values = with_chains(first, chain, chain_row, pair, embed, wide, step)
     start[...] = values
-    centred, rstd = stats(values)
-    normed = (centred * rstd * column(gain[...])).astype(BF16)
-    normed_out[...] = normed
-    send[:, :, window(step)] = gated_pair(pm, dot_tn(proj[...], normed))
-
-
-def gate_kernel(normed, gate, gated):
-    gated[...] = sigmoid(dot_tn(gate[...], normed[...]))
+    gated[...] = sigmoid(dot_tn(gate[...], normed_by(values, gain)))
 
 
 def middle_kernel(
@@ -126,6 +145,7 @@
     wide,
 ):
     step = pl.program_id(0)
+    hold(first, "middle", step)
     pm = tile_mask(first, mask, mask_row, wide, step)
     centred, rstd = stats(xs[:, :, window(step)].astype(F32).reshape(CH, TILE))
     y = (centred * rstd * column(mid_gain[...])).astype(BF16)
@@ -148,7 +168,7 @@
     rounded = scaled.astype(BF16)
     grad_value[...] = rounded
     factor[...] = scaled * (1.0 - sigma)
-    grad_h[...] = dot_nn(final[...], rounded) * column(gain[...])
+    grad_h[...] = (dot_nn(final[...], rounded) * column(gain[...])).astype(BF16)
     p = dot_tn(proj[...], normed)
     for side in range(2):
         low = 2 * side * CH
@@ -161,7 +181,7 @@
 def turn_kernel(xs, grad_h, send):
     step = pl.program_id(0)
     centred, rstd = stats(xs[:, :, window(step)].astype(F32).reshape(CH, TILE))
-    grad_x = norm_grad(centred * rstd, rstd, grad_h[...])
+    grad_x = norm_grad(centred * rstd, rstd, grad_h[...].astype(F32))
     send[:, :, window(step)] = grad_x.astype(BF16).reshape(DEVS, CPD, TILE)
 
 
@@ -185,20 +205,25 @@
     sums[:, 2 * CH :] += lane_sums(grad_y * hat)
 
 
-def last_kernel(gs, in_normed, factors, sums, grad_p, packed, acc_proj):
-    step = pl.program_id(0)
+def grad_of_proj(gs, factors, step):
     grads = gs[:, :, window(step)].astype(F32).reshape(DEVS, 2, CPD, TILE)
+    parts = []
     for side in range(2):
         grad = grads[:, side].reshape(CH, TILE)
         for part in range(2):
             low = (2 * side + part) * CH
-            grad_p[low : low + CH, :] = (grad * factors[low : low + CH, :].astype(F32)).astype(BF16)
+            parts.append((grad * factors[low : low + CH, :].astype(F32)).astype(BF16))
+    return jnp.concatenate(parts, axis=0)
+
+
+def last_kernel(gs, in_normed, factors, sums, packed, acc_proj):
+    step = pl.program_id(0)
 
     @pl.when(step == 0)
     def _():
         acc_proj[...] = jnp.zeros_like(acc_proj)
 
-    acc_proj[...] += dot_nt(in_normed[...], grad_p[...])
+    acc_proj[...] += dot_nt(in_normed[...], grad_of_proj(gs, factors, step))
 
     @pl.when(step == STEPS - 1)
     def _():
@@ -206,9 +231,9 @@
         packed[...] = (full * (1.0 / RES)).astype(BF16).reshape(DEVS, CPD, GCOLS)
 
 
-def norm_kernel(cot, pair_mid, grad_p, from_gate, gain, proj, sums, pair_grad, gains, acc):
-    step = pl.program_id(0)
-    grad_normed = dot_nn(proj[...], grad_p[...]) + from_gate[...]
+def norm_kernel(cot, pair_mid, gs, factors, from_gate, gain, proj, sums, pair_grad, gains, acc):
+    step = pl.program_id(0)
+    grad_normed = dot_nn(proj[...], grad_of_proj(gs, factors, step)) + from_gate[...]
     centred, rstd = stats(pair_mid[...].astype(F32))
     hat = centred * rstd
     grad_z = norm_grad(hat, rstd, grad_normed * column(gain[...]))
@@ -296,7 +321,8 @@
             flat[pl.ds((3 * q + h) * rows + c, DEVS, stride=width), :] = tiles[h]
 
 
-def outgoing_kernel(recv, send, flat, mats_a, mats_b, out):
+def outgoing_kernel(first, recv, send, flat, mats_a, mats_b, out):
+    hold(first, "outgoing")
     unfold(recv, flat, 2 * CPD)
     for c in range(CPD):
         a = gather_matrix(flat, 2 * CPD, c, mats_a.at[c])
@@ -316,8 +342,11 @@
     fold(out, send, CPD)
 
 
-def backward_kernel(recv, sides, send, flat, mats_a, mats_b, out):
+def backward_kernel(recv, sides_far, send, flat, mats_a, mats_b, out, sides, sem):
+    fetch = pltpu.make_async_copy(sides_far, sides, sem)
+    fetch.start()
     unfold(recv, flat, CPD)
+    fetch.wait()
     for c in range(CPD):
         g = gather_matrix(flat, CPD, c, mats_a.at[c])
         scatter_matrix(dot_nt(sides[CPD + c], g), mats_a.at[c], out, 2 * CPD, c)
@@ -325,22 +354,24 @@
     fold(out, send, 2 * CPD)
 
 
-def product(kernel, args, out_shape, width_in, width_out, name):
+SMEM = pl.BlockSpec(memory_space=pltpu.SMEM)
+HERE = pl.BlockSpec(memory_space=pltpu.VMEM)
+
+
+def product(kernel, args, out_shape, width_in, width_out, name, in_specs=None, extra=()):
     return pl.pallas_call(
         kernel,
         out_shape=out_shape,
+        in_specs=[HERE] if in_specs is None else in_specs,
         scratch_shapes=[
             pltpu.VMEM((LTILES * DEVS * width_in, LANES), F32),
             pltpu.VMEM((CPD, 2 * RES, LANES), F32),
             pltpu.VMEM((CPD, 2 * RES, LANES), F32),
             pltpu.VMEM((LTILES * DEVS * width_out, LANES), F32),
+            *extra,
         ],
         name=name,
     )(*args)
-
-
-SMEM = pl.BlockSpec(memory_space=pltpu.SMEM)
-HERE = pl.BlockSpec(memory_space=pltpu.VMEM)
 
 
 def whole(shape):
@@ -402,7 +433,7 @@
     in_mid_gain,
     in_final,
 ):
-    first = (lax.axis_index(AXIS) * ROWS).astype(jnp.int32).reshape(1)
+    first = jnp.stack([lax.axis_index(AXIS) * ROWS, lax.axis_index("cplx") % 2]).astype(jnp.int32)
     mask_row, chain_row = residue_mask.reshape(1, RES), chain_ids.reshape(1, RES)
     gains = [g.reshape(1, CH) for g in (out_norm_gain, out_mid_gain, in_norm_gain, in_mid_gain)]
     pair_send = near((DEVS, 2 * CPD, POS))
@@ -410,20 +441,27 @@
     cols = shaped((CH, POS))
     cols_f32 = shaped((CH, POS), F32)
 
-    send, start, out_normed = over_tiles(
+    chains = (first, chain_ids, chain_row, pair, chain_embed, gains[0])
+    (send,) = over_tiles(
         first_kernel,
         (first, residue_mask, chain_ids, mask_row, chain_row, pair, chain_embed, gains[0], out_proj),
         [SMEM, SMEM, SMEM, LANE_INFO, LANE_INFO, ROW_BLOCK, whole((2, CH)), GAIN, WIDE],
-        [HERE, COLS, COLS],
-        [pair_send, cols_f32, cols],
+        [HERE],
+        [pair_send],
         "first",
         WIDE_ROW,
     )
     recv = exchange(send)
-    gated = over_tiles(
-        gate_kernel, (out_normed, out_gate), [COLS, SQUARE], COLS, cols_f32, "gate"
-    )
-    x_out = product(outgoing_kernel, (recv,), one_send, 2 * CPD, CPD, "outgoing")
+    start, gated = over_tiles(
+        gate_kernel,
+        (*chains, out_gate),
+        [SMEM, SMEM, LANE_INFO, ROW_BLOCK, whole((2, CH)), GAIN, SQUARE],
+        [COLS, COLS],
+        [cols_f32, cols_f32],
+        "gate",
+        WIDE_ROW,
+    )
+    x_out = product(outgoing_kernel, (first, recv), one_send, 2 * CPD, CPD, "outgoing", [SMEM, HERE])
     send, pair_mid, in_normed = over_tiles(
         middle_kernel,
         (first, residue_mask, mask_row, exchange(x_out), start, gated, gains[1], out_final, gains[2], in_proj),
@@ -439,14 +477,14 @@
         (first, residue_mask, mask_row, cotangent, in_normed, gains[3], in_gate, in_final, in_proj),
         [SMEM, SMEM, LANE_INFO, ROW_BLOCK, COLS, GAIN, SQUARE, SQUARE, WIDE],
         [COLS, COLS, COLS, tiled(4 * CH)],
-        [cols, cols_f32, cols_f32, shaped((4 * CH, POS))],
+        [cols, cols, cols_f32, shaped((4 * CH, POS))],
         "ahead",
         WIDE_ROW,
     )
     x_in, sides = product(
         incoming_kernel,
         (recv,),
-        [one_send, near((2 * CPD, RES, RES))],
+        [one_send, shaped((2 * CPD, RES, RES))],
         2 * CPD,
         CPD,
         "incoming",
@@ -462,21 +500,24 @@
         [shaped((CH, 3 * CH), F32), cols_f32],
         "after",
     )
-    grads = product(backward_kernel, (recv_x, sides), pair_send, CPD, 2 * CPD, "backward")
-    grad_p, packed = over_tiles(
+    grads = product(backward_kernel, (recv_x, sides), pair_send, CPD, 2 * CPD, "backward",
+                    [HERE, pl.BlockSpec(memory_space=pl.ANY)],
+                    [pltpu.VMEM((2 * CPD, RES, RES), BF16), pltpu.SemaphoreType.DMA])
+    gs = exchange(grads)
+    (packed,) = over_tiles(
         last_kernel,
-        (exchange(grads), in_normed, factors, sums),
+        (gs, in_normed, factors, sums),
         [HERE, COLS, tiled(4 * CH), whole((CH, 3 * CH))],
-        [tiled(4 * CH), HERE],
-        [shaped((4 * CH, POS)), near((DEVS, CPD, GCOLS))],
+        [HERE],
+        [near((DEVS, CPD, GCOLS))],
         "last",
         [pltpu.VMEM((CH, 4 * CH), F32)],
     )
     parts = exchange(packed)
     pair_grad, gain_rows = over_tiles(
         norm_kernel,
-        (cotangent, pair_mid, grad_p, from_gate, gains[2], in_proj, sums),
-        [ROW_BLOCK, COLS, tiled(4 * CH), COLS, GAIN, WIDE, whole((CH, 3 * CH))],
+        (cotangent, pair_mid, gs, factors, from_gate, gains[2], in_proj, sums),
+        [ROW_BLOCK, COLS, HERE, tiled(4 * CH), COLS, GAIN, WIDE, whole((CH, 3 * CH))],
         [ROW_BLOCK, whole((CPD, CH))],
         [shaped((ROWS, RES, CH)), shaped((CPD, CH), F32)],
         "norm",

time: 221 us -> 186 us (0.84)
  blocking collectives: 106 us -> 75.2 us
  waiting for transfers between devices: 56.8 us -> 35.9 us
  Pallas kernels: 39.5 us -> 58.1 us
    all_to_all x4, blocking collectives: 106 us -> 75.2 us  [exchange(): lax.all_to_all(v, AXIS, 0, 0)]
    all_to_all x4, waiting for transfers between devices: 56.8 us -> 35.9 us  [exchange(): lax.all_to_all(v, AXIS, 0, 0)]
    pallas_call x8, Pallas kernels: 27.9 us -> 45.4 us  [over_tiles(): pl.pallas_call(kernel, grid=(STEPS,), in_specs=in_specs, out_specs=out_sp...]
  transfers between devices with their start and end apart: 4 -> 4, of which waited for: 4 -> 4; matrix products, arithmetic and copies ran while one was open for 0% -> 0% of each run, Pallas kernels for 7% -> 9%
where the time goes in v3:
time: 186 us; the launch traced here: 185 us
  blocking collectives  75.2 us (40%)
  Pallas kernels  58.1 us (31%)
  waiting for transfers between devices  35.9 us (19%)
  starting transfers between devices  14.4 us (8%)
    all_to_all x4, blocking collectives, exchange(): lax.all_to_all(v, AXIS, 0, 0)  75.2 us
    pallas_call x8, Pallas kernels, over_tiles(): pl.pallas_call(kernel, grid=(STEPS,), in_specs=in_specs, out_specs=out_sp...  45.4 us
    all_to_all x4, waiting for transfers between devices, exchange(): lax.all_to_all(v, AXIS, 0, 0)  35.9 us
    all_to_all x4, starting transfers between devices, exchange(): lax.all_to_all(v, AXIS, 0, 0)  14.4 us
    pallas_call x3, Pallas kernels, product(): pl.pallas_call(kernel, out_shape=out_shape, in_specs=[HERE] if in_specs i...  11.3 us
  transfers between devices with their start and end apart: 4, of which 4 were waited for; matrix products, arithmetic and copies ran while one was open for 0% of the time, Pallas kernels for 9%

profile of v3, /device:TPU:1, one launch (start us, length us, event | category | flops | bytes accessed | tf_op | source)
XLA Modules:
  0.0 184.9 jit_solution(4686278695739562847)
XLA Ops:
  1.2 17.2 %first.1 = bf16[16,16,2304]{2,1,0:T(8,128)(2,1)S(1)} custom-call(s32[2]{0:T(128)} %pad_add_fusion.first, s32[192]{0:T(256)} %mask.5, s32[192]{0:T(256)} %chain.3, s32[1,192]{1,0:T(1,128)} %bitcast.14, s32[1,192]{1,0:T(1,128)} %bitcast.12, bf16[12,192,128]{2,1,0:T(8,128)(2,1)} %pair.3, f32[2,128]{1,0:T(2,128)} %embed.3, f32[1,128]{1,0:T(1,128)} %bitcast.17, ...), custom_call_target="tpu_custom_call" | custom-call | flops 1073741824 | bytes 4194304 | tf_op jit(solution)/shard_map/first/pallas_call | solution.py:395
  18.4 27.0 %all_to_all.40.recv = bf16[16,16,2304]{2,1,0:T(8,128)(2,1)S(1)} all-to-all(bf16[16,16,2304]{2,1,0:T(8,128)(2,1)S(1)} %first.1), channel_id=1, replica_groups=mesh['dap'=16,'cplx'=16] {'dap'}, dimensions={0} | all-to-all | bytes 2359296 | tf_op jit(solution)/shard_map/all_to_all | solution.py:416
  45.4 3.1 %outgoing.1 = bf16[16,8,2304]{2,1,0:T(8,128)(2,1)} custom-call(s32[2]{0:T(128)} %pad_add_fusion.first, bf16[16,16,2304]{2,1,0:T(8,128)(2,1)S(1)} %all_to_all.40.recv), custom_call_target="tpu_custom_call" | custom-call | tf_op jit(solution)/shard_map/outgoing/pallas_call | solution.py:362
  48.5 3.6 %all-to-all-start.1 = ((bf16[16,8,2304]{2,1,0:T(8,128)(2,1)}), bf16[16,8,2304]{2,1,0:T(8,128)(2,1)S(1)}, u32[]{:S(2)}, u32[]{:S(2)}) async-start(bf16[16,8,2304]{2,1,0:T(8,128)(2,1)} %outgoing.1), calls=%async_computation.1 | async-start | bytes 1179648 | tf_op jit(solution)/shard_map/all_to_all | solution.py:416
  52.1 3.0 %gate.4 = (f32[128,2304]{1,0:T(8,128)}, f32[128,2304]{1,0:T(8,128)}) custom-call(s32[2]{0:T(128)} %pad_add_fusion.first, s32[192]{0:T(256)} %chain.3, s32[1,192]{1,0:T(1,128)} %bitcast.13, bf16[12,192,128]{2,1,0:T(8,128)(2,1)} %pair.3, f32[2,128]{1,0:T(2,128)} %embed.3, f32[1,128]{1,0:T(1,128)} %bitcast.18, bf16[128,128]{1,0:T(8,128)(2,1)} %gate.5), custom_call_target="tpu_custom_call" | custom-call | flops 1073741824 | bytes 4194304 | tf_op jit(solution)/shard_map/gate/pallas_call | solution.py:395
  55.1 8.8 %all-to-all-done.1.xs = bf16[16,8,2304]{2,1,0:T(8,128)(2,1)S(1)} async-done(((bf16[16,8,2304]{2,1,0:T(8,128)(2,1)}), bf16[16,8,2304]{2,1,0:T(8,128)(2,1)S(1)}, u32[]{:S(2)}, u32[]{:S(2)}) %all-to-all-start.1) | async-done | bytes 589856 | tf_op jit(solution)/shard_map/all_to_all | solution.py:416
  63.9 7.4 %middle.1 = (bf16[16,16,2304]{2,1,0:T(8,128)(2,1)S(1)}, bf16[128,2304]{1,0:T(8,128)(2,1)}, bf16[128,2304]{1,0:T(8,128)(2,1)}) custom-call(s32[2]{0:T(128)} %pad_add_fusion.first, s32[192]{0:T(256)} %mask.5, s32[1,192]{1,0:T(1,128)} %bitcast.15, bf16[16,8,2304]{2,1,0:T(8,128)(2,1)S(1)} %all-to-all-done.1.xs, f32[128,2304]{1,0:T(8,128)} %get-tuple-element.26.start, ...), custom_call_target="tpu_custom_call" | custom-call | flops 1073741824 | bytes 4194304 | tf_op jit(solution)/shard_map/middle/pallas_call | solution.py:395
  71.3 20.8 %all_to_all.41.recv = bf16[16,16,2304]{2,1,0:T(8,128)(2,1)S(1)} all-to-all(bf16[16,16,2304]{2,1,0:T(8,128)(2,1)S(1)} %get-tuple-element.29), channel_id=1, replica_groups=mesh['dap'=16,'cplx'=16] {'dap'}, dimensions={0} | all-to-all | bytes 2359296 | tf_op jit(solution)/shard_map/all_to_all | solution.py:416
  92.1 4.1 %incoming.1 = (bf16[16,8,2304]{2,1,0:T(8,128)(2,1)}, bf16[16,192,192]{2,1,0:T(8,128)(2,1)}) custom-call(bf16[16,16,2304]{2,1,0:T(8,128)(2,1)S(1)} %all_to_all.41.recv), custom_call_target="tpu_custom_call" | custom-call | tf_op jit(solution)/shard_map/incoming/pallas_call | solution.py:362
  96.2 3.6 %all-to-all-start.3 = ((bf16[16,8,2304]{2,1,0:T(8,128)(2,1)}), bf16[16,8,2304]{2,1,0:T(8,128)(2,1)S(1)}, u32[]{:S(2)}, u32[]{:S(2)}) async-start(bf16[16,8,2304]{2,1,0:T(8,128)(2,1)} %get-tuple-element.30), calls=%async_computation.3 | async-start | bytes 1179648 | tf_op jit(solution)/shard_map/all_to_all | solution.py:416
  99.8 4.3 %ahead.1 = (bf16[128,2304]{1,0:T(8,128)(2,1)}, bf16[128,2304]{1,0:T(8,128)(2,1)}, f32[128,2304]{1,0:T(8,128)}, bf16[512,2304]{1,0:T(8,128)(2,1)}) custom-call(s32[2]{0:T(128)} %pad_add_fusion.first, s32[192]{0:T(256)} %mask.5, s32[1,192]{1,0:T(1,128)} %bitcast.16, bf16[12,192,128]{2,1,0:T(8,128)(2,1)} %cot.3, bf16[128,2304]{1,0:T(8,128)(2,1)} %get-tuple-element.31.in_normed, ...), custom_call_target="tpu_custom_call" | custom-call | flops 1073741824 | bytes 4194304 | tf_op jit(solution)/shard_map/ahead/pallas_call | solution.py:395
  104.0 8.2 %all-to-all-done.3.xs = bf16[16,8,2304]{2,1,0:T(8,128)(2,1)S(1)} async-done(((bf16[16,8,2304]{2,1,0:T(8,128)(2,1)}), bf16[16,8,2304]{2,1,0:T(8,128)(2,1)S(1)}, u32[]{:S(2)}, u32[]{:S(2)}) %all-to-all-start.3) | async-done | bytes 589856 | tf_op jit(solution)/shard_map/all_to_all | solution.py:416
  112.2 1.8 turn.1
  114.0 16.0 %all_to_all.42.recv = bf16[16,8,2304]{2,1,0:T(8,128)(2,1)S(1)} all-to-all(bf16[16,8,2304]{2,1,0:T(8,128)(2,1)S(1)} %turn.1), channel_id=1, replica_groups=mesh['dap'=16,'cplx'=16] {'dap'}, dimensions={0} | all-to-all | bytes 1179648 | tf_op jit(solution)/shard_map/all_to_all | solution.py:416
  129.9 4.1 %backward.1 = bf16[16,16,2304]{2,1,0:T(8,128)(2,1)} custom-call(bf16[16,8,2304]{2,1,0:T(8,128)(2,1)S(1)} %all_to_all.42.recv, bf16[16,192,192]{2,1,0:T(8,128)(2,1)} %get-tuple-element.33.sides_far), custom_call_target="tpu_custom_call" | custom-call | tf_op jit(solution)/shard_map/backward/pallas_call | solution.py:362
  134.1 3.7 %all-to-all-start.5 = ((bf16[16,16,2304]{2,1,0:T(8,128)(2,1)}), bf16[16,16,2304]{2,1,0:T(8,128)(2,1)S(1)}, u32[]{:S(2)}, u32[]{:S(2)}) async-start(bf16[16,16,2304]{2,1,0:T(8,128)(2,1)} %backward.1), calls=%async_computation.5 | async-start | bytes 2359296 | tf_op jit(solution)/shard_map/all_to_all | solution.py:416
  137.8 4.0 %after.1 = (f32[128,384]{1,0:T(8,128)}, f32[128,2304]{1,0:T(8,128)}) custom-call(bf16[16,8,2304]{2,1,0:T(8,128)(2,1)S(1)} %all-to-all-done.3.xs, bf16[128,2304]{1,0:T(8,128)(2,1)} %get-tuple-element.31.in_normed, bf16[128,2304]{1,0:T(8,128)(2,1)} %get-tuple-element.35.grad_value, f32[128,2304]{1,0:T(8,128)} %get-tuple-element.36.factor, f32[1,128]{1,0:T(1,128)} %bitcast.21, ...), custom_call_target="tpu_custom_call" | custom-call | flops 1073741824 | bytes 4194304 | tf_op jit(solution)/shard_map/after/pallas_call | solution.py:395
  141.8 16.0 %all-to-all-done.5.gs = bf16[16,16,2304]{2,1,0:T(8,128)(2,1)S(1)} async-done(((bf16[16,16,2304]{2,1,0:T(8,128)(2,1)}), bf16[16,16,2304]{2,1,0:T(8,128)(2,1)S(1)}, u32[]{:S(2)}, u32[]{:S(2)}) %all-to-all-start.5) | async-done | bytes 1179680 | tf_op jit(solution)/shard_map/all_to_all | solution.py:416
  157.7 3.2 %last.1 = bf16[16,8,768]{2,1,0:T(8,128)(2,1)} custom-call(bf16[16,16,2304]{2,1,0:T(8,128)(2,1)S(1)} %all-to-all-done.5.gs, bf16[128,2304]{1,0:T(8,128)(2,1)} %get-tuple-element.31.in_normed, bf16[512,2304]{1,0:T(8,128)(2,1)} %get-tuple-element.34.factors, f32[128,384]{1,0:T(8,128)} %get-tuple-element.38.sums), custom_call_target="tpu_custom_call" | custom-call | flops 1073741824 | bytes 4194304 | tf_op jit(solution)/shard_map/last/pallas_call | solution.py:395
  161.0 3.5 %all-to-all-start.6 = ((bf16[16,8,768]{2,1,0:T(8,128)(2,1)}), bf16[16,8,768]{2,1,0:T(8,128)(2,1)S(1)}, u32[]{:S(2)}, u32[]{:S(2)}) async-start(bf16[16,8,768]{2,1,0:T(8,128)(2,1)} %last.1), calls=%async_computation.6 | async-start | bytes 393216 | tf_op jit(solution)/shard_map/all_to_all | solution.py:416
  164.5 4.5 %norm.1 = (bf16[12,192,128]{2,1,0:T(8,128)(2,1)}, f32[8,128]{1,0:T(8,128)}) custom-call(bf16[12,192,128]{2,1,0:T(8,128)(2,1)} %cot.3, bf16[128,2304]{1,0:T(8,128)(2,1)} %get-tuple-element.28.pair_mid, bf16[16,16,2304]{2,1,0:T(8,128)(2,1)S(1)} %all-to-all-done.5.gs, bf16[512,2304]{1,0:T(8,128)(2,1)} %get-tuple-element.34.factors, ...), custom_call_target="tpu_custom_call" | custom-call | flops 1073741824 | bytes 4194304 | tf_op jit(solution)/shard_map/norm/pallas_call | solution.py:395
  169.1 2.9 %all-to-all-done.6.parts = bf16[16,8,768]{2,1,0:T(8,128)(2,1)S(1)} async-done(((bf16[16,8,768]{2,1,0:T(8,128)(2,1)}), bf16[16,8,768]{2,1,0:T(8,128)(2,1)S(1)}, u32[]{:S(2)}, u32[]{:S(2)}) %all-to-all-start.6) | async-done | bytes 196640 | tf_op jit(solution)/shard_map/all_to_all | solution.py:416
  172.7 11.4 %all_to_all.43.parts = bf16[16,8,896]{2,1,0:T(8,128)(2,1)S(1)} all-to-all(bf16[16,8,896]{2,1,0:T(8,128)(2,1)S(1)} %add.8), channel_id=1, replica_groups=mesh['dap'=16,'cplx'=16] {'dap'}, dimensions={0} | all-to-all | bytes 458752 | tf_op jit(solution)/shard_map/all_to_all | solution.py:416
  184.2 0.8 unpack.1
  (2 shorter events, 1.3 us)
Async XLA Ops:
  48.5 15.4 %all-to-all-start.1 = ((bf16[16,8,2304]{2,1,0:T(8,128)(2,1)}), bf16[16,8,2304]{2,1,0:T(8,128)(2,1)S(1)}, u32[]{:S(2)}, u32[]{:S(2)}) async-start(bf16[16,8,2304]{2,1,0:T(8,128)(2,1)} %outgoing.1), calls=%async_computation.1 | async-start | bytes 1179648 | tf_op jit(solution)/shard_map/all_to_all | solution.py:416
  96.2 16.0 %all-to-all-start.3 = ((bf16[16,8,2304]{2,1,0:T(8,128)(2,1)}), bf16[16,8,2304]{2,1,0:T(8,128)(2,1)S(1)}, u32[]{:S(2)}, u32[]{:S(2)}) async-start(bf16[16,8,2304]{2,1,0:T(8,128)(2,1)} %get-tuple-element.30), calls=%async_computation.3 | async-start | bytes 1179648 | tf_op jit(solution)/shard_map/all_to_all | solution.py:416
  134.1 23.7 %all-to-all-start.5 = ((bf16[16,16,2304]{2,1,0:T(8,128)(2,1)}), bf16[16,16,2304]{2,1,0:T(8,128)(2,1)S(1)}, u32[]{:S(2)}, u32[]{:S(2)}) async-start(bf16[16,16,2304]{2,1,0:T(8,128)(2,1)} %backward.1), calls=%async_computation.5 | async-start | bytes 2359296 | tf_op jit(solution)/shard_map/all_to_all | solution.py:416
  161.0 11.0 %all-to-all-start.6 = ((bf16[16,8,768]{2,1,0:T(8,128)(2,1)}), bf16[16,8,768]{2,1,0:T(8,128)(2,1)S(1)}, u32[]{:S(2)}, u32[]{:S(2)}) async-start(bf16[16,8,768]{2,1,0:T(8,128)(2,1)} %last.1), calls=%async_computation.6 | async-start | bytes 393216 | tf_op jit(solution)/shard_map/all_to_all | solution.py:416

commit v4 on v3

--- a/solution.py
+++ b/solution.py
@@ -20,7 +20,7 @@
 LANES = 128
 LTILES = POS // LANES
 GCOLS = 6 * CH
-HOLD_NS = {"first": (0, 14700), "outgoing": (1000, 0), "middle": (0, 3600)}
+HOLD_NS = {"first": (0, 14500), "outgoing": (2000, 0), "middle": (0, 4500)}
 EPS = 1e-05
 
 
@@ -62,7 +62,7 @@
 
 
 def tile_rows(first_ref, table_ref, step):
-    base = first_ref[0] + TROWS * step
+    base = (first_ref[0] >> 1) + TROWS * step
     lane = lax.broadcasted_iota(jnp.int32, (1, TILE), 1)
     out = jnp.full((1, TILE), table_ref[base], jnp.int32)
     for r in range(1, TROWS):
@@ -107,7 +107,7 @@
     for core, nanos in enumerate(HOLD_NS[name]):
         if nanos:
 
-            @pl.when((step == 0) & (first_ref[1] == core))
+            @pl.when((step == 0) & ((first_ref[0] & 1) == core))
             def _():
                 pl.delay(nanos)
 
@@ -433,7 +433,8 @@
     in_mid_gain,
     in_final,
 ):
-    first = jnp.stack([lax.axis_index(AXIS) * ROWS, lax.axis_index("cplx") % 2]).astype(jnp.int32)
+    first = lax.axis_index(AXIS) * (2 * ROWS) + lax.axis_index("cplx") % 2
+    first = first.astype(jnp.int32).reshape(1)
     mask_row, chain_row = residue_mask.reshape(1, RES), chain_ids.reshape(1, RES)
     gains = [g.reshape(1, CH) for g in (out_norm_gain, out_mid_gain, in_norm_gain, in_mid_gain)]
     pair_send = near((DEVS, 2 * CPD, POS))

time: 186 us -> 185 us (level)
  no operation moved by 1% of the time
where the time goes in v4:
time: 185 us
  blocking collectives  75.4 us (41%)
  Pallas kernels  58.1 us (31%)
  waiting for transfers between devices  35.9 us (19%)
  starting transfers between devices  14.4 us (8%)
    all_to_all x4, blocking collectives, exchange(): lax.all_to_all(v, AXIS, 0, 0)  75.4 us
    pallas_call x8, Pallas kernels, over_tiles(): pl.pallas_call(kernel, grid=(STEPS,), in_specs=in_specs, out_specs=out_sp...  46 us
    all_to_all x4, waiting for transfers between devices, exchange(): lax.all_to_all(v, AXIS, 0, 0)  35.9 us
    all_to_all x4, starting transfers between devices, exchange(): lax.all_to_all(v, AXIS, 0, 0)  14.4 us
    pallas_call x3, Pallas kernels, product(): pl.pallas_call(kernel, out_shape=out_shape, in_specs=[HERE] if in_specs i...  10.6 us
  transfers between devices with their start and end apart: 4, of which 4 were waited for; matrix products, arithmetic and copies ran while one was open for 0% of the time, Pallas kernels for 9%

profile of v4, /device:TPU:1, one launch (start us, length us, event | category | flops | bytes accessed | tf_op | source)
XLA Modules:
  0.0 184.6 jit_solution(11443673415056338858)
XLA Ops:
  0.6 17.0 %first.1 = bf16[16,16,2304]{2,1,0:T(8,128)(2,1)S(1)} custom-call(s32[1]{0:T(128)} %bitcast.first, s32[192]{0:T(256)} %mask.5, s32[192]{0:T(256)} %chain.3, s32[1,192]{1,0:T(1,128)} %bitcast.13, s32[1,192]{1,0:T(1,128)} %bitcast.11, bf16[12,192,128]{2,1,0:T(8,128)(2,1)} %pair.3, f32[2,128]{1,0:T(2,128)} %embed.3, f32[1,128]{1,0:T(1,128)} %bitcast.16, ...), custom_call_target="tpu_custom_call" | custom-call | flops 1073741824 | bytes 4194304 | tf_op jit(solution)/shard_map/first/pallas_call | solution.py:395
  17.7 27.1 %all_to_all.40.recv = bf16[16,16,2304]{2,1,0:T(8,128)(2,1)S(1)} all-to-all(bf16[16,16,2304]{2,1,0:T(8,128)(2,1)S(1)} %first.1), channel_id=1, replica_groups=mesh['dap'=16,'cplx'=16] {'dap'}, dimensions={0} | all-to-all | bytes 2359296 | tf_op jit(solution)/shard_map/all_to_all | solution.py:416
  44.8 2.4 %outgoing.1 = bf16[16,8,2304]{2,1,0:T(8,128)(2,1)} custom-call(s32[1]{0:T(128)} %bitcast.first, bf16[16,16,2304]{2,1,0:T(8,128)(2,1)S(1)} %all_to_all.40.recv), custom_call_target="tpu_custom_call" | custom-call | tf_op jit(solution)/shard_map/outgoing/pallas_call | solution.py:362
  47.2 3.6 %all-to-all-start.1 = ((bf16[16,8,2304]{2,1,0:T(8,128)(2,1)}), bf16[16,8,2304]{2,1,0:T(8,128)(2,1)S(1)}, u32[]{:S(2)}, u32[]{:S(2)}) async-start(bf16[16,8,2304]{2,1,0:T(8,128)(2,1)} %outgoing.1), calls=%async_computation.1 | async-start | bytes 1179648 | tf_op jit(solution)/shard_map/all_to_all | solution.py:416
  50.7 3.0 %gate.4 = (f32[128,2304]{1,0:T(8,128)}, f32[128,2304]{1,0:T(8,128)}) custom-call(s32[1]{0:T(128)} %bitcast.first, s32[192]{0:T(256)} %chain.3, s32[1,192]{1,0:T(1,128)} %bitcast.12, bf16[12,192,128]{2,1,0:T(8,128)(2,1)} %pair.3, f32[2,128]{1,0:T(2,128)} %embed.3, f32[1,128]{1,0:T(1,128)} %bitcast.17, bf16[128,128]{1,0:T(8,128)(2,1)} %gate.5), custom_call_target="tpu_custom_call" | custom-call | flops 1073741824 | bytes 4194304 | tf_op jit(solution)/shard_map/gate/pallas_call | solution.py:395
  53.7 8.8 %all-to-all-done.1.xs = bf16[16,8,2304]{2,1,0:T(8,128)(2,1)S(1)} async-done(((bf16[16,8,2304]{2,1,0:T(8,128)(2,1)}), bf16[16,8,2304]{2,1,0:T(8,128)(2,1)S(1)}, u32[]{:S(2)}, u32[]{:S(2)}) %all-to-all-start.1) | async-done | bytes 589856 | tf_op jit(solution)/shard_map/all_to_all | solution.py:416
  62.6 8.3 %middle.1 = (bf16[16,16,2304]{2,1,0:T(8,128)(2,1)S(1)}, bf16[128,2304]{1,0:T(8,128)(2,1)}, bf16[128,2304]{1,0:T(8,128)(2,1)}) custom-call(s32[1]{0:T(128)} %bitcast.first, s32[192]{0:T(256)} %mask.5, s32[1,192]{1,0:T(1,128)} %bitcast.14, bf16[16,8,2304]{2,1,0:T(8,128)(2,1)S(1)} %all-to-all-done.1.xs, f32[128,2304]{1,0:T(8,128)} %get-tuple-element.26.start, ...), custom_call_target="tpu_custom_call" | custom-call | flops 1073741824 | bytes 4194304 | tf_op jit(solution)/shard_map/middle/pallas_call | solution.py:395
  70.8 20.9 %all_to_all.41.recv = bf16[16,16,2304]{2,1,0:T(8,128)(2,1)S(1)} all-to-all(bf16[16,16,2304]{2,1,0:T(8,128)(2,1)S(1)} %get-tuple-element.29), channel_id=1, replica_groups=mesh['dap'=16,'cplx'=16] {'dap'}, dimensions={0} | all-to-all | bytes 2359296 | tf_op jit(solution)/shard_map/all_to_all | solution.py:416
  91.7 4.1 %incoming.1 = (bf16[16,8,2304]{2,1,0:T(8,128)(2,1)}, bf16[16,192,192]{2,1,0:T(8,128)(2,1)}) custom-call(bf16[16,16,2304]{2,1,0:T(8,128)(2,1)S(1)} %all_to_all.41.recv), custom_call_target="tpu_custom_call" | custom-call | tf_op jit(solution)/shard_map/incoming/pallas_call | solution.py:362
  95.8 3.6 %all-to-all-start.3 = ((bf16[16,8,2304]{2,1,0:T(8,128)(2,1)}), bf16[16,8,2304]{2,1,0:T(8,128)(2,1)S(1)}, u32[]{:S(2)}, u32[]{:S(2)}) async-start(bf16[16,8,2304]{2,1,0:T(8,128)(2,1)} %get-tuple-element.30), calls=%async_computation.3 | async-start | bytes 1179648 | tf_op jit(solution)/shard_map/all_to_all | solution.py:416
  99.4 4.3 %ahead.1 = (bf16[128,2304]{1,0:T(8,128)(2,1)}, bf16[128,2304]{1,0:T(8,128)(2,1)}, f32[128,2304]{1,0:T(8,128)}, bf16[512,2304]{1,0:T(8,128)(2,1)}) custom-call(s32[1]{0:T(128)} %bitcast.first, s32[192]{0:T(256)} %mask.5, s32[1,192]{1,0:T(1,128)} %bitcast.15, bf16[12,192,128]{2,1,0:T(8,128)(2,1)} %cot.3, bf16[128,2304]{1,0:T(8,128)(2,1)} %get-tuple-element.31.in_normed, ...), custom_call_target="tpu_custom_call" | custom-call | flops 1073741824 | bytes 4194304 | tf_op jit(solution)/shard_map/ahead/pallas_call | solution.py:395
  103.7 8.1 %all-to-all-done.3.xs = bf16[16,8,2304]{2,1,0:T(8,128)(2,1)S(1)} async-done(((bf16[16,8,2304]{2,1,0:T(8,128)(2,1)}), bf16[16,8,2304]{2,1,0:T(8,128)(2,1)S(1)}, u32[]{:S(2)}, u32[]{:S(2)}) %all-to-all-start.3) | async-done | bytes 589856 | tf_op jit(solution)/shard_map/all_to_all | solution.py:416
  111.8 1.8 turn.1
  113.6 16.0 %all_to_all.42.recv = bf16[16,8,2304]{2,1,0:T(8,128)(2,1)S(1)} all-to-all(bf16[16,8,2304]{2,1,0:T(8,128)(2,1)S(1)} %turn.1), channel_id=1, replica_groups=mesh['dap'=16,'cplx'=16] {'dap'}, dimensions={0} | all-to-all | bytes 1179648 | tf_op jit(solution)/shard_map/all_to_all | solution.py:416
  129.5 4.1 %backward.1 = bf16[16,16,2304]{2,1,0:T(8,128)(2,1)} custom-call(bf16[16,8,2304]{2,1,0:T(8,128)(2,1)S(1)} %all_to_all.42.recv, bf16[16,192,192]{2,1,0:T(8,128)(2,1)} %get-tuple-element.33.sides_far), custom_call_target="tpu_custom_call" | custom-call | tf_op jit(solution)/shard_map/backward/pallas_call | solution.py:362
  133.7 3.7 %all-to-all-start.5 = ((bf16[16,16,2304]{2,1,0:T(8,128)(2,1)}), bf16[16,16,2304]{2,1,0:T(8,128)(2,1)S(1)}, u32[]{:S(2)}, u32[]{:S(2)}) async-start(bf16[16,16,2304]{2,1,0:T(8,128)(2,1)} %backward.1), calls=%async_computation.5 | async-start | bytes 2359296 | tf_op jit(solution)/shard_map/all_to_all | solution.py:416
  137.4 4.0 %after.1 = (f32[128,384]{1,0:T(8,128)}, f32[128,2304]{1,0:T(8,128)}) custom-call(bf16[16,8,2304]{2,1,0:T(8,128)(2,1)S(1)} %all-to-all-done.3.xs, bf16[128,2304]{1,0:T(8,128)(2,1)} %get-tuple-element.31.in_normed, bf16[128,2304]{1,0:T(8,128)(2,1)} %get-tuple-element.35.grad_value, f32[128,2304]{1,0:T(8,128)} %get-tuple-element.36.factor, f32[1,128]{1,0:T(1,128)} %bitcast.20, ...), custom_call_target="tpu_custom_call" | custom-call | flops 1073741824 | bytes 4194304 | tf_op jit(solution)/shard_map/after/pallas_call | solution.py:395
  141.4 16.0 %all-to-all-done.5.gs = bf16[16,16,2304]{2,1,0:T(8,128)(2,1)S(1)} async-done(((bf16[16,16,2304]{2,1,0:T(8,128)(2,1)}), bf16[16,16,2304]{2,1,0:T(8,128)(2,1)S(1)}, u32[]{:S(2)}, u32[]{:S(2)}) %all-to-all-start.5) | async-done | bytes 1179680 | tf_op jit(solution)/shard_map/all_to_all | solution.py:416
  157.4 3.2 %last.1 = bf16[16,8,768]{2,1,0:T(8,128)(2,1)} custom-call(bf16[16,16,2304]{2,1,0:T(8,128)(2,1)S(1)} %all-to-all-done.5.gs, bf16[128,2304]{1,0:T(8,128)(2,1)} %get-tuple-element.31.in_normed, bf16[512,2304]{1,0:T(8,128)(2,1)} %get-tuple-element.34.factors, f32[128,384]{1,0:T(8,128)} %get-tuple-element.38.sums), custom_call_target="tpu_custom_call" | custom-call | flops 1073741824 | bytes 4194304 | tf_op jit(solution)/shard_map/last/pallas_call | solution.py:395
  160.6 3.5 %all-to-all-start.6 = ((bf16[16,8,768]{2,1,0:T(8,128)(2,1)}), bf16[16,8,768]{2,1,0:T(8,128)(2,1)S(1)}, u32[]{:S(2)}, u32[]{:S(2)}) async-start(bf16[16,8,768]{2,1,0:T(8,128)(2,1)} %last.1), calls=%async_computation.6 | async-start | bytes 393216 | tf_op jit(solution)/shard_map/all_to_all | solution.py:416
  164.2 4.5 %norm.1 = (bf16[12,192,128]{2,1,0:T(8,128)(2,1)}, f32[8,128]{1,0:T(8,128)}) custom-call(bf16[12,192,128]{2,1,0:T(8,128)(2,1)} %cot.3, bf16[128,2304]{1,0:T(8,128)(2,1)} %get-tuple-element.28.pair_mid, bf16[16,16,2304]{2,1,0:T(8,128)(2,1)S(1)} %all-to-all-done.5.gs, bf16[512,2304]{1,0:T(8,128)(2,1)} %get-tuple-element.34.factors, ...), custom_call_target="tpu_custom_call" | custom-call | flops 1073741824 | bytes 4194304 | tf_op jit(solution)/shard_map/norm/pallas_call | solution.py:395
  168.7 2.9 %all-to-all-done.6.parts = bf16[16,8,768]{2,1,0:T(8,128)(2,1)S(1)} async-done(((bf16[16,8,768]{2,1,0:T(8,128)(2,1)}), bf16[16,8,768]{2,1,0:T(8,128)(2,1)S(1)}, u32[]{:S(2)}, u32[]{:S(2)}) %all-to-all-start.6) | async-done | bytes 196640 | tf_op jit(solution)/shard_map/all_to_all | solution.py:416
  172.3 11.4 %all_to_all.43.parts = bf16[16,8,896]{2,1,0:T(8,128)(2,1)S(1)} all-to-all(bf16[16,8,896]{2,1,0:T(8,128)(2,1)S(1)} %add.10), channel_id=1, replica_groups=mesh['dap'=16,'cplx'=16] {'dap'}, dimensions={0} | all-to-all | bytes 458752 | tf_op jit(solution)/shard_map/all_to_all | solution.py:416
  183.8 0.8 unpack.1
  (1 shorter events, 0.7 us)
Async XLA Ops:
  47.2 15.4 %all-to-all-start.1 = ((bf16[16,8,2304]{2,1,0:T(8,128)(2,1)}), bf16[16,8,2304]{2,1,0:T(8,128)(2,1)S(1)}, u32[]{:S(2)}, u32[]{:S(2)}) async-start(bf16[16,8,2304]{2,1,0:T(8,128)(2,1)} %outgoing.1), calls=%async_computation.1 | async-start | bytes 1179648 | tf_op jit(solution)/shard_map/all_to_all | solution.py:416
  95.8 16.0 %all-to-all-start.3 = ((bf16[16,8,2304]{2,1,0:T(8,128)(2,1)}), bf16[16,8,2304]{2,1,0:T(8,128)(2,1)S(1)}, u32[]{:S(2)}, u32[]{:S(2)}) async-start(bf16[16,8,2304]{2,1,0:T(8,128)(2,1)} %get-tuple-element.30), calls=%async_computation.3 | async-start | bytes 1179648 | tf_op jit(solution)/shard_map/all_to_all | solution.py:416
  133.7 23.7 %all-to-all-start.5 = ((bf16[16,16,2304]{2,1,0:T(8,128)(2,1)}), bf16[16,16,2304]{2,1,0:T(8,128)(2,1)S(1)}, u32[]{:S(2)}, u32[]{:S(2)}) async-start(bf16[16,16,2304]{2,1,0:T(8,128)(2,1)} %backward.1), calls=%async_computation.5 | async-start | bytes 2359296 | tf_op jit(solution)/shard_map/all_to_all | solution.py:416
  160.6 11.0 %all-to-all-start.6 = ((bf16[16,8,768]{2,1,0:T(8,128)(2,1)}), bf16[16,8,768]{2,1,0:T(8,128)(2,1)S(1)}, u32[]{:S(2)}, u32[]{:S(2)}) async-start(bf16[16,8,768]{2,1,0:T(8,128)(2,1)} %last.1), calls=%async_computation.6 | async-start | bytes 393216 | tf_op jit(solution)/shard_map/all_to_all | solution.py:416

commit v5 on v4

--- a/solution.py
+++ b/solution.py
@@ -20,7 +20,7 @@
 LANES = 128
 LTILES = POS // LANES
 GCOLS = 6 * CH
-HOLD_NS = {"first": (0, 14500), "outgoing": (2000, 0), "middle": (0, 4500)}
+HOLD_NS = {"first": (0, 14500), "outgoing": (1000, 0), "middle": (0, 3500)}
 EPS = 1e-05
 
 

time: 185 us -> 184 us (level)
  no operation moved by 1% of the time
where the time goes in v5:
time: 184 us
  blocking collectives  75.9 us (41%)
  Pallas kernels  57.1 us (31%)
  waiting for transfers between devices  35.5 us (19%)
  starting transfers between devices  14.4 us (8%)
    all_to_all x4, blocking collectives, exchange(): lax.all_to_all(v, AXIS, 0, 0)  75.9 us
    pallas_call x8, Pallas kernels, over_tiles(): pl.pallas_call(kernel, grid=(STEPS,), in_specs=in_specs, out_specs=out_sp...  45 us
    all_to_all x4, waiting for transfers between devices, exchange(): lax.all_to_all(v, AXIS, 0, 0)  35.5 us
    all_to_all x4, starting transfers between devices, exchange(): lax.all_to_all(v, AXIS, 0, 0)  14.4 us
    pallas_call x3, Pallas kernels, product(): pl.pallas_call(kernel, out_shape=out_shape, in_specs=[HERE] if in_specs i...  10.6 us
  transfers between devices with their start and end apart: 4, of which 4 were waited for; matrix products, arithmetic and copies ran while one was open for 0% of the time, Pallas kernels for 9%

profile of v5, /device:TPU:1, one launch (start us, length us, event | category | flops | bytes accessed | tf_op | source)
XLA Modules:
  0.0 183.5 jit_solution(12291738152544703493)
XLA Ops:
  0.6 17.0 %first.1 = bf16[16,16,2304]{2,1,0:T(8,128)(2,1)S(1)} custom-call(s32[1]{0:T(128)} %bitcast.first, s32[192]{0:T(256)} %mask.5, s32[192]{0:T(256)} %chain.3, s32[1,192]{1,0:T(1,128)} %bitcast.13, s32[1,192]{1,0:T(1,128)} %bitcast.11, bf16[12,192,128]{2,1,0:T(8,128)(2,1)} %pair.3, f32[2,128]{1,0:T(2,128)} %embed.3, f32[1,128]{1,0:T(1,128)} %bitcast.16, ...), custom_call_target="tpu_custom_call" | custom-call | flops 1073741824 | bytes 4194304 | tf_op jit(solution)/shard_map/first/pallas_call | solution.py:395
  17.7 27.1 %all_to_all.40.recv = bf16[16,16,2304]{2,1,0:T(8,128)(2,1)S(1)} all-to-all(bf16[16,16,2304]{2,1,0:T(8,128)(2,1)S(1)} %first.1), channel_id=1, replica_groups=mesh['dap'=16,'cplx'=16] {'dap'}, dimensions={0} | all-to-all | bytes 2359296 | tf_op jit(solution)/shard_map/all_to_all | solution.py:416
  44.8 2.4 %outgoing.1 = bf16[16,8,2304]{2,1,0:T(8,128)(2,1)} custom-call(s32[1]{0:T(128)} %bitcast.first, bf16[16,16,2304]{2,1,0:T(8,128)(2,1)S(1)} %all_to_all.40.recv), custom_call_target="tpu_custom_call" | custom-call | tf_op jit(solution)/shard_map/outgoing/pallas_call | solution.py:362
  47.2 3.6 %all-to-all-start.1 = ((bf16[16,8,2304]{2,1,0:T(8,128)(2,1)}), bf16[16,8,2304]{2,1,0:T(8,128)(2,1)S(1)}, u32[]{:S(2)}, u32[]{:S(2)}) async-start(bf16[16,8,2304]{2,1,0:T(8,128)(2,1)} %outgoing.1), calls=%async_computation.1 | async-start | bytes 1179648 | tf_op jit(solution)/shard_map/all_to_all | solution.py:416
  50.8 3.0 %gate.4 = (f32[128,2304]{1,0:T(8,128)}, f32[128,2304]{1,0:T(8,128)}) custom-call(s32[1]{0:T(128)} %bitcast.first, s32[192]{0:T(256)} %chain.3, s32[1,192]{1,0:T(1,128)} %bitcast.12, bf16[12,192,128]{2,1,0:T(8,128)(2,1)} %pair.3, f32[2,128]{1,0:T(2,128)} %embed.3, f32[1,128]{1,0:T(1,128)} %bitcast.17, bf16[128,128]{1,0:T(8,128)(2,1)} %gate.5), custom_call_target="tpu_custom_call" | custom-call | flops 1073741824 | bytes 4194304 | tf_op jit(solution)/shard_map/gate/pallas_call | solution.py:395
  53.8 8.8 %all-to-all-done.1.xs = bf16[16,8,2304]{2,1,0:T(8,128)(2,1)S(1)} async-done(((bf16[16,8,2304]{2,1,0:T(8,128)(2,1)}), bf16[16,8,2304]{2,1,0:T(8,128)(2,1)S(1)}, u32[]{:S(2)}, u32[]{:S(2)}) %all-to-all-start.1) | async-done | bytes 589856 | tf_op jit(solution)/shard_map/all_to_all | solution.py:416
  62.6 7.3 %middle.1 = (bf16[16,16,2304]{2,1,0:T(8,128)(2,1)S(1)}, bf16[128,2304]{1,0:T(8,128)(2,1)}, bf16[128,2304]{1,0:T(8,128)(2,1)}) custom-call(s32[1]{0:T(128)} %bitcast.first, s32[192]{0:T(256)} %mask.5, s32[1,192]{1,0:T(1,128)} %bitcast.14, bf16[16,8,2304]{2,1,0:T(8,128)(2,1)S(1)} %all-to-all-done.1.xs, f32[128,2304]{1,0:T(8,128)} %get-tuple-element.26.start, ...), custom_call_target="tpu_custom_call" | custom-call | flops 1073741824 | bytes 4194304 | tf_op jit(solution)/shard_map/middle/pallas_call | solution.py:395
  69.9 20.9 %all_to_all.41.recv = bf16[16,16,2304]{2,1,0:T(8,128)(2,1)S(1)} all-to-all(bf16[16,16,2304]{2,1,0:T(8,128)(2,1)S(1)} %get-tuple-element.29), channel_id=1, replica_groups=mesh['dap'=16,'cplx'=16] {'dap'}, dimensions={0} | all-to-all | bytes 2359296 | tf_op jit(solution)/shard_map/all_to_all | solution.py:416
  90.8 4.1 %incoming.1 = (bf16[16,8,2304]{2,1,0:T(8,128)(2,1)}, bf16[16,192,192]{2,1,0:T(8,128)(2,1)}) custom-call(bf16[16,16,2304]{2,1,0:T(8,128)(2,1)S(1)} %all_to_all.41.recv), custom_call_target="tpu_custom_call" | custom-call | tf_op jit(solution)/shard_map/incoming/pallas_call | solution.py:362
  94.8 3.6 %all-to-all-start.3 = ((bf16[16,8,2304]{2,1,0:T(8,128)(2,1)}), bf16[16,8,2304]{2,1,0:T(8,128)(2,1)S(1)}, u32[]{:S(2)}, u32[]{:S(2)}) async-start(bf16[16,8,2304]{2,1,0:T(8,128)(2,1)} %get-tuple-element.30), calls=%async_computation.3 | async-start | bytes 1179648 | tf_op jit(solution)/shard_map/all_to_all | solution.py:416
  98.4 4.3 %ahead.1 = (bf16[128,2304]{1,0:T(8,128)(2,1)}, bf16[128,2304]{1,0:T(8,128)(2,1)}, f32[128,2304]{1,0:T(8,128)}, bf16[512,2304]{1,0:T(8,128)(2,1)}) custom-call(s32[1]{0:T(128)} %bitcast.first, s32[192]{0:T(256)} %mask.5, s32[1,192]{1,0:T(1,128)} %bitcast.15, bf16[12,192,128]{2,1,0:T(8,128)(2,1)} %cot.3, bf16[128,2304]{1,0:T(8,128)(2,1)} %get-tuple-element.31.in_normed, ...), custom_call_target="tpu_custom_call" | custom-call | flops 1073741824 | bytes 4194304 | tf_op jit(solution)/shard_map/ahead/pallas_call | solution.py:395
  102.7 8.2 %all-to-all-done.3.xs = bf16[16,8,2304]{2,1,0:T(8,128)(2,1)S(1)} async-done(((bf16[16,8,2304]{2,1,0:T(8,128)(2,1)}), bf16[16,8,2304]{2,1,0:T(8,128)(2,1)S(1)}, u32[]{:S(2)}, u32[]{:S(2)}) %all-to-all-start.3) | async-done | bytes 589856 | tf_op jit(solution)/shard_map/all_to_all | solution.py:416
  110.9 1.8 turn.1
  112.7 16.4 %all_to_all.42.recv = bf16[16,8,2304]{2,1,0:T(8,128)(2,1)S(1)} all-to-all(bf16[16,8,2304]{2,1,0:T(8,128)(2,1)S(1)} %turn.1), channel_id=1, replica_groups=mesh['dap'=16,'cplx'=16] {'dap'}, dimensions={0} | all-to-all | bytes 1179648 | tf_op jit(solution)/shard_map/all_to_all | solution.py:416
  129.0 4.2 %backward.1 = bf16[16,16,2304]{2,1,0:T(8,128)(2,1)} custom-call(bf16[16,8,2304]{2,1,0:T(8,128)(2,1)S(1)} %all_to_all.42.recv, bf16[16,192,192]{2,1,0:T(8,128)(2,1)} %get-tuple-element.33.sides_far), custom_call_target="tpu_custom_call" | custom-call | tf_op jit(solution)/shard_map/backward/pallas_call | solution.py:362
  133.2 3.7 %all-to-all-start.5 = ((bf16[16,16,2304]{2,1,0:T(8,128)(2,1)}), bf16[16,16,2304]{2,1,0:T(8,128)(2,1)S(1)}, u32[]{:S(2)}, u32[]{:S(2)}) async-start(bf16[16,16,2304]{2,1,0:T(8,128)(2,1)} %backward.1), calls=%async_computation.5 | async-start | bytes 2359296 | tf_op jit(solution)/shard_map/all_to_all | solution.py:416
  136.9 4.0 %after.1 = (f32[128,384]{1,0:T(8,128)}, f32[128,2304]{1,0:T(8,128)}) custom-call(bf16[16,8,2304]{2,1,0:T(8,128)(2,1)S(1)} %all-to-all-done.3.xs, bf16[128,2304]{1,0:T(8,128)(2,1)} %get-tuple-element.31.in_normed, bf16[128,2304]{1,0:T(8,128)(2,1)} %get-tuple-element.35.grad_value, f32[128,2304]{1,0:T(8,128)} %get-tuple-element.36.factor, f32[1,128]{1,0:T(1,128)} %bitcast.20, ...), custom_call_target="tpu_custom_call" | custom-call | flops 1073741824 | bytes 4194304 | tf_op jit(solution)/shard_map/after/pallas_call | solution.py:395
  140.9 15.5 %all-to-all-done.5.gs = bf16[16,16,2304]{2,1,0:T(8,128)(2,1)S(1)} async-done(((bf16[16,16,2304]{2,1,0:T(8,128)(2,1)}), bf16[16,16,2304]{2,1,0:T(8,128)(2,1)S(1)}, u32[]{:S(2)}, u32[]{:S(2)}) %all-to-all-start.5) | async-done | bytes 1179680 | tf_op jit(solution)/shard_map/all_to_all | solution.py:416
  156.4 3.2 %last.1 = bf16[16,8,768]{2,1,0:T(8,128)(2,1)} custom-call(bf16[16,16,2304]{2,1,0:T(8,128)(2,1)S(1)} %all-to-all-done.5.gs, bf16[128,2304]{1,0:T(8,128)(2,1)} %get-tuple-element.31.in_normed, bf16[512,2304]{1,0:T(8,128)(2,1)} %get-tuple-element.34.factors, f32[128,384]{1,0:T(8,128)} %get-tuple-element.38.sums), custom_call_target="tpu_custom_call" | custom-call | flops 1073741824 | bytes 4194304 | tf_op jit(solution)/shard_map/last/pallas_call | solution.py:395
  159.6 3.5 %all-to-all-start.6 = ((bf16[16,8,768]{2,1,0:T(8,128)(2,1)}), bf16[16,8,768]{2,1,0:T(8,128)(2,1)S(1)}, u32[]{:S(2)}, u32[]{:S(2)}) async-start(bf16[16,8,768]{2,1,0:T(8,128)(2,1)} %last.1), calls=%async_computation.6 | async-start | bytes 393216 | tf_op jit(solution)/shard_map/all_to_all | solution.py:416
  163.2 4.5 %norm.1 = (bf16[12,192,128]{2,1,0:T(8,128)(2,1)}, f32[8,128]{1,0:T(8,128)}) custom-call(bf16[12,192,128]{2,1,0:T(8,128)(2,1)} %cot.3, bf16[128,2304]{1,0:T(8,128)(2,1)} %get-tuple-element.28.pair_mid, bf16[16,16,2304]{2,1,0:T(8,128)(2,1)S(1)} %all-to-all-done.5.gs, bf16[512,2304]{1,0:T(8,128)(2,1)} %get-tuple-element.34.factors, ...), custom_call_target="tpu_custom_call" | custom-call | flops 1073741824 | bytes 4194304 | tf_op jit(solution)/shard_map/norm/pallas_call | solution.py:395
  167.7 2.9 %all-to-all-done.6.parts = bf16[16,8,768]{2,1,0:T(8,128)(2,1)S(1)} async-done(((bf16[16,8,768]{2,1,0:T(8,128)(2,1)}), bf16[16,8,768]{2,1,0:T(8,128)(2,1)S(1)}, u32[]{:S(2)}, u32[]{:S(2)}) %all-to-all-start.6) | async-done | bytes 196640 | tf_op jit(solution)/shard_map/all_to_all | solution.py:416
  171.3 11.4 %all_to_all.43.parts = bf16[16,8,896]{2,1,0:T(8,128)(2,1)S(1)} all-to-all(bf16[16,8,896]{2,1,0:T(8,128)(2,1)S(1)} %add.10), channel_id=1, replica_groups=mesh['dap'=16,'cplx'=16] {'dap'}, dimensions={0} | all-to-all | bytes 458752 | tf_op jit(solution)/shard_map/all_to_all | solution.py:416
  182.8 0.8 unpack.1
  (1 shorter events, 0.7 us)
Async XLA Ops:
  47.2 15.4 %all-to-all-start.1 = ((bf16[16,8,2304]{2,1,0:T(8,128)(2,1)}), bf16[16,8,2304]{2,1,0:T(8,128)(2,1)S(1)}, u32[]{:S(2)}, u32[]{:S(2)}) async-start(bf16[16,8,2304]{2,1,0:T(8,128)(2,1)} %outgoing.1), calls=%async_computation.1 | async-start | bytes 1179648 | tf_op jit(solution)/shard_map/all_to_all | solution.py:416
  94.8 16.1 %all-to-all-start.3 = ((bf16[16,8,2304]{2,1,0:T(8,128)(2,1)}), bf16[16,8,2304]{2,1,0:T(8,128)(2,1)S(1)}, u32[]{:S(2)}, u32[]{:S(2)}) async-start(bf16[16,8,2304]{2,1,0:T(8,128)(2,1)} %get-tuple-element.30), calls=%async_computation.3 | async-start | bytes 1179648 | tf_op jit(solution)/shard_map/all_to_all | solution.py:416
  133.2 23.2 %all-to-all-start.5 = ((bf16[16,16,2304]{2,1,0:T(8,128)(2,1)}), bf16[16,16,2304]{2,1,0:T(8,128)(2,1)S(1)}, u32[]{:S(2)}, u32[]{:S(2)}) async-start(bf16[16,16,2304]{2,1,0:T(8,128)(2,1)} %backward.1), calls=%async_computation.5 | async-start | bytes 2359296 | tf_op jit(solution)/shard_map/all_to_all | solution.py:416
  159.6 11.0 %all-to-all-start.6 = ((bf16[16,8,768]{2,1,0:T(8,128)(2,1)}), bf16[16,8,768]{2,1,0:T(8,128)(2,1)S(1)}, u32[]{:S(2)}, u32[]{:S(2)}) async-start(bf16[16,8,768]{2,1,0:T(8,128)(2,1)} %last.1), calls=%async_computation.6 | async-start | bytes 393216 | tf_op jit(solution)/shard_map/all_to_all | solution.py:416
